TPU v7x, 512 devices: a whole 4x8x8 slice. The times are simulated.
512 devices in a mesh: expert: 32 (over z, y_hi), tensor: 16 (over y_lo, x, core).
Axes of the slice: x: 4, y: 8 (y_hi: 4, y_lo: 2; y = y_hi * 2 + y_lo), z: 8, core: 2. Of those that a mesh axis runs over, the one named last changes fastest.
Arguments:
- tokens: bfloat16 [4096, 3072], P('expert', 'tensor'), may hold values from -6 to 6
- expert_ids: int32 [4096, 2], P('expert'), may hold values from 0 to 7, all different within a row; in each aligned block of 128 rows (0 to 127, 128 to 255, ...) at most 48 rows name the same one
- joined_weight: bfloat16 [32, 3072, 2, 4096], P('expert', 'tensor'), may hold values from -0.109375 to 0.109375
Outputs:
- hidden: bfloat16 [4096, 2, 4, 4096], P('expert', None, None, 'tensor')
Inputs may be any that keep to these rules, and one draw needn't show every extreme that they name: `expert_ids`: each row names 2 different experts. Among the rows of one device (each aligned block of 128 rows) no expert is named by more than 48 rows, and in some blocks one expert is named by exactly 48 rows.
All inputs are finite; a program needn't handle non-finite values.
Results may differ from a plain program's by a relative error of at most 0.001.
Values may be sent and summed in bfloat16 or wider, within the bound.
No kernel may reach another device: no remote copies, remote signals or barrier semaphores. Data moves between devices by JAX's collectives and lax.ppermute only.
A program may use at most 128 MiB of HBM per device.

v0:
```python
import jax
import jax.numpy as jnp
from jax import lax
from jax.sharding import PartitionSpec as P

E = 8
TOP = 2
CAP = 48


def activate(gate_up, half_width):
    gate = gate_up[:, :half_width]
    upward = gate_up[:, half_width:]
    return (jax.nn.silu(gate) * upward).astype(jnp.bfloat16)


def give_back(active):
    return lax.all_to_all(active, "expert", split_axis=0, concat_axis=0, tiled=True)


def local(tokens, expert_ids, joined_weight):
    groups = lax.axis_size("tensor")
    blocks = lax.axis_size("expert")
    copies = blocks // E
    local_rows = joined_weight.shape[1]
    half_width = joined_weight.shape[3] // groups
    pieces = joined_weight[0].reshape(local_rows, 2, groups, half_width)
    arranged = lax.all_to_all(pieces, "tensor", split_axis=2, concat_axis=0, tiled=True)
    weights = arranged.reshape(local_rows * groups, 2 * half_width)
    tok_count = tokens.shape[0]
    flat_ids = expert_ids.reshape(-1)
    chosen = (flat_ids[:, None] == jnp.arange(E, dtype=jnp.int32)[None, :]).astype(jnp.int32)
    earlier = jnp.cumsum(chosen, axis=0) - chosen
    position = jnp.sum(earlier * chosen, axis=1)
    slot_index = flat_ids * CAP + position
    pick_table = (slot_index[:, None] == jnp.arange(E * CAP, dtype=jnp.int32)[None, :]).astype(
        jnp.bfloat16
    )
    token_table = pick_table.reshape(tok_count, TOP, E * CAP).sum(axis=1)
    width = tokens.shape[1]
    placed = lax.dot_general(
        token_table, tokens, (((0,), (0,)), ((), ())), preferred_element_type=jnp.float32
    )
    placed = placed.astype(jnp.bfloat16).reshape(E, 1, CAP, width)
    outgoing = jnp.broadcast_to(placed, (E, copies, CAP, width)).reshape(blocks, CAP, width)
    received = lax.all_to_all(outgoing, "expert", split_axis=0, concat_axis=0, tiled=True)
    slot_count = received.shape[1]
    piece = lax.all_gather(received, "tensor", axis=2, tiled=True)
    row_block = piece.reshape(blocks * slot_count, piece.shape[2])
    gate_up = jnp.dot(row_block, weights, preferred_element_type=jnp.float32)
    returned = give_back(activate(gate_up, half_width).reshape(blocks, slot_count, half_width))
    grouped = (
        returned.reshape(E, copies, CAP, half_width)
        .transpose(0, 2, 1, 3)
        .reshape(E * CAP, copies * half_width)
    )
    hidden = jnp.dot(pick_table, grouped, preferred_element_type=jnp.float32).astype(jnp.bfloat16)
    return hidden.reshape(tok_count, TOP, copies, half_width)


def solution(mesh):
    placed = (P("expert", "tensor"), P("expert", None), P("expert", "tensor", None, None))
    return jax.shard_map(
        local,
        mesh=mesh,
        in_specs=placed,
        out_specs=P("expert", None, None, "tensor"),
        check_vma=False,
    )
```

profile of v0, /device:TPU:10, one launch (start us, length us, event | category | flops | bytes accessed | tf_op | source)
XLA Modules:
  0.0 299.9 jit_solution(4116273108823073041)
XLA Ops:
  6.5 0.0 copy-start
  6.5 0.0 all-gather.2.cloned.1.call-start
  6.5 0.8 copy.55
  7.3 0.1 reshape.62
  7.5 0.1 eq.46
  7.6 0.6 reduce-window.6
  8.2 0.2 slice_reduce_fusion
  8.5 0.1 fusion.5
  8.6 0.1 reduce_sum.24
  8.7 0.1 copy.57
  8.8 0.7 multiply_add_fusion
  9.5 0.1 fusion.2
  9.6 0.0 copy-done
  9.6 0.2 convolution_convert_fusion.1
  9.8 0.1 copy.58
  9.9 0.1 broadcast_in_dim.5
  10.0 37.4 %all_to_all.25 = bf16[32,48,192]{2,1,0:T(8,128)(2,1)S(1)} all-to-all(bf16[32,48,192]{2,1,0:T(8,128)(2,1)S(1)} %bitcast.36), channel_id=1, replica_groups=mesh['expert'=32,'tensor'=16] {'expert'}, dimensions={0} | all-to-all | bytes 1179648 | tf_op jit(solution)/shard_map/all_to_all | solution.py:46
  47.4 2.3 copy.59
  49.7 0.0 all-gather.2.cloned.1.call-update
  49.7 4.6 %reshape_squeeze.3 = bf16[192,2,16,256]{3,2,1,0:T(8,128)(2,1)S(1)} reshape(bf16[1,192,2,4096]{3,2,1,0:T(2,128)(2,1)} %param.5) | data formatting | bytes 6291456 | tf_op jit(solution)/shard_map/reshape;squeeze | solution.py:27
  54.3 3.0 %copy.61 = bf16[192,2,16,256]{3,1,0,2:T(2,128)(2,1)S(1)} copy(bf16[192,2,16,256]{3,2,1,0:T(8,128)(2,1)S(1)} %reshape_squeeze.3) | data formatting | bytes 6291456 | tf_op jit(solution)/shard_map/reshape;squeeze | solution.py:27
  57.3 75.2 %all_to_all.26 = bf16[192,2,16,256]{3,1,0,2:T(2,128)(2,1)S(1)} all-to-all(bf16[192,2,16,256]{3,1,0,2:T(2,128)(2,1)S(1)} %copy.61), channel_id=1, replica_groups=mesh['expert'=32,'tensor'=16] {'tensor'}, dimensions={2} | all-to-all | bytes 6291456 | tf_op jit(solution)/shard_map/all_to_all | solution.py:28
  132.5 0.5 copy.63
  133.1 86.2 %all-gather.2.cloned.1.call-done = bf16[32,48,3072]{1,0,2:T(8,128)(2,1)} async-done(((bf16[32,48,192]{1,0,2:T(8,128)(2,1)}), bf16[32,48,3072]{1,0,2:T(8,128)(2,1)}) %all-gather.2.cloned.1.call-update) | async-done | bytes 9437200 | tf_op jit(solution)/shard_map/all_gather | solution.py:48
  219.3 26.3 %copy.60 = bf16[32,48,3072]{2,1,0:T(8,128)(2,1)} copy(bf16[32,48,3072]{1,0,2:T(8,128)(2,1)} %all-gather.2.cloned.1.call-done) | data formatting | bytes 18874368 | tf_op jit(solution)/shard_map/all_gather | solution.py:48
  245.5 7.5 %fusion.7 = f32[1536,512]{1,0:T(8,128)S(1)} fusion(bf16[1536,3072]{1,0:T(8,128)(2,1)} %bitcast.31, bf16[3072,512]{1,0:T(8,128)(2,1)S(1)} %bitcast.32), kind=kOutput, calls=%fused_computation.18 | convolution fusion | flops 4831838208 | bytes 15728640 | tf_op jit(solution)/shard_map/dot_general | solution.py:50
  253.1 1.3 fusion
  254.4 9.7 %all-to-all-start.2 = ((bf16[32,48,256]{2,1,0:T(8,128)(2,1)}), bf16[32,48,256]{2,1,0:T(8,128)(2,1)S(1)}, u32[]{:S(2)}, u32[]{:S(2)}) async-start(bf16[32,48,256]{2,1,0:T(8,128)(2,1)} %bitcast.7), calls=%async_computation.2 | async-start | bytes 1572864 | tf_op jit(solution)/shard_map/all_to_all | solution.py:18
  264.1 26.8 %all-to-all-done.2 = bf16[32,48,256]{2,1,0:T(8,128)(2,1)S(1)} async-done(((bf16[32,48,256]{2,1,0:T(8,128)(2,1)}), bf16[32,48,256]{2,1,0:T(8,128)(2,1)S(1)}, u32[]{:S(2)}, u32[]{:S(2)}) %all-to-all-start.2) | async-done | bytes 786464 | tf_op jit(solution)/shard_map/all_to_all | solution.py:18
  290.8 0.4 copy.62
  291.3 0.2 copy.64
  291.4 0.5 convolution_convert_fusion
  291.9 1.2 reshape.70
  (4 shorter events, 0.1 us)
Async XLA Ops:
  6.5 3.1 %copy-start = (bf16[128,192]{0,1:T(8,128)(2,1)S(1)}, bf16[128,192]{0,1:T(8,128)(2,1)}, u32[]{:S(2)}) copy-start(bf16[128,192]{0,1:T(8,128)(2,1)} %param.3) | copy-start | bytes 147460
  6.5 212.7 %all-gather.2.cloned.1.call-start = ((), (), s32[]{:S(2)}) async-start(), calls=%async_computation.3 | async-start | bytes 26738688 | tf_op jit(solution)/shard_map/all_gather | solution.py:48
  254.4 36.5 %all-to-all-start.2 = ((bf16[32,48,256]{2,1,0:T(8,128)(2,1)}), bf16[32,48,256]{2,1,0:T(8,128)(2,1)S(1)}, u32[]{:S(2)}, u32[]{:S(2)}) async-start(bf16[32,48,256]{2,1,0:T(8,128)(2,1)} %bitcast.7), calls=%async_computation.2 | async-start | bytes 1572864 | tf_op jit(solution)/shard_map/all_to_all | solution.py:18
Sparse Core Ops, SparseCore 0:
  49.8 169.3 all-gather.1
where the time goes:
time: 301 us; the launch traced here: 300 us
  blocking collectives  113 us (38%)
  waiting for transfers between devices  113 us (38%)
  local copies, waits for them, and re-layouts  40.1 us (13%)
  between operations  13.5 us (4%)
  starting transfers between devices  9.68 us (3%)
  matrix products  8.2 us (3%)
    all_gather x1, waiting for transfers between devices, local(): piece = lax.all_gather(received, 'tensor', axis=2, tiled=True)  86.2 us
    all_to_all x1, blocking collectives, local(): lax.all_to_all(pieces, 'tensor', split_axis=2, concat_axis=0, tiled=True)  75.2 us
    all_to_all x1, blocking collectives, local(): lax.all_to_all(outgoing, 'expert', split_axis=0, concat_axis=0, tiled=True)  37.4 us
    all_to_all x1, waiting for transfers between devices, give_back(): lax.all_to_all(active, 'expert', split_axis=0, concat_axis=0, tiled=True)  26.8 us
    all_gather x1, local copies, waits for them, and re-layouts, local(): piece = lax.all_gather(received, 'tensor', axis=2, tiled=True)  26.3 us
    all_to_all x1, starting transfers between devices, give_back(): lax.all_to_all(active, 'expert', split_axis=0, concat_axis=0, tiled=True)  9.68 us
    another operation x2, local copies, waits for them, and re-layouts, local(): pieces = joined_weight[0].reshape(local_rows, 2, groups, half_width)  7.59 us
    dot_general x1, matrix products, local(): gate_up = jnp.dot(row_block, weights, preferred_element_type=jnp.float32)  7.53 us
  transfers between devices with their start and end apart: 2, of which 2 were waited for; matrix products, arithmetic and copies ran while one was open for 3% of the time, Pallas kernels for 0%

commit v1 on v0

v1 whole, which is shorter than its diff:
```python
import jax
import jax.numpy as jnp
from jax import lax
from jax.experimental import pallas as pl
from jax.experimental.pallas import tpu as pltpu
from jax.sharding import Mesh, PartitionSpec as P

E = 8
TOP = 2
CAP = 48
GROUPS = ((0,), (1, 3), (2,))


EXPERT = ("z", "yh")
TENSOR = ("yl", "x", "c")
SWAP = [(0, 1), (1, 0)]


def shift(axis, by):
    n = lax.axis_size(axis)
    return [(i, (i + by) % n) for i in range(n)]


def split_kernel(w_ref, out_ref, sems):
    chips, width = out_ref.shape[0], out_ref.shape[3]
    copies = [
        pltpu.make_async_copy(
            w_ref.at[0, :, :, pl.ds(p * width, width)], out_ref.at[p], sems.at[p]
        )
        for p in range(chips)
    ]
    for copy in copies:
        copy.start()
    for copy in copies:
        copy.wait()


def split_columns(joined_weight, chips):
    _, rows, two, columns = joined_weight.shape
    shape = (chips, rows, two, columns // chips)
    return pl.pallas_call(
        split_kernel,
        out_shape=jax.ShapeDtypeStruct(shape, joined_weight.dtype),
        in_specs=[pl.BlockSpec(memory_space=pl.ANY)],
        out_specs=pl.BlockSpec(memory_space=pltpu.VMEM),
        scratch_shapes=[pltpu.SemaphoreType.DMA((chips,))],
        cost_estimate=pl.CostEstimate(flops=10**9, bytes_accessed=2 * 3 * 2**20, transcendentals=0),
        compiler_params=pltpu.CompilerParams(vmem_limit_bytes=8 * 2**20),
    )(joined_weight)


def hidden_kernel(groups, place, w_own, w_other, *refs):
    pieces, out = refs[: 5 * len(groups)], refs[-1]
    zs, cores, xs = 8, 2, 4
    n, half_width = out.shape[1], out.shape[2]
    height = zs * n
    depth = w_own.shape[0] // (2 * xs)
    for g, members in enumerate(groups):
        own, low, high, far_a, far_b = pieces[5 * g : 5 * g + 5]
        cut = far_a.shape[0]
        for i, m in enumerate(members):
            start, stop = i * height, (i + 1) * height
            rows = slice(start, stop)
            if stop <= cut:
                far = far_a[rows]
            elif start >= cut:
                far = far_b[start - cut : stop - cut]
            else:
                far = jnp.concatenate([far_a[start:cut], far_b[: stop - cut]], axis=0)
            for w, c in ((w_own, place[4]), (w_other, place[5])):
                total = jnp.zeros((height, 2 * half_width), jnp.float32)
                for k, x in enumerate((own[rows], low[rows], high[rows], far)):
                    for side in range(2):
                        at = pl.multiple_of((side * xs + place[k]) * depth, depth)
                        total = total + jnp.dot(
                            x[:, side * depth : (side + 1) * depth],
                            w[pl.ds(at, depth)],
                            preferred_element_type=jnp.float32,
                        )
                gate, up = total[:, :half_width], total[:, half_width:]
                active = (gate / (1.0 + jnp.exp(-gate)) * up).astype(jnp.bfloat16)
                for z in range(zs):
                    out[place[6 + m] * (zs * cores) + place[10 + z] * cores + c] = active[
                        z * n : (z + 1) * n
                    ]


def hidden_blocks(place, pieces, w_own, w_other, groups, n, half_width, held=None):
    vmem = pl.BlockSpec(memory_space=pltpu.VMEM)
    pieces = [p for group in pieces for p in group]
    inputs = [place, w_own, w_other] + pieces + ([] if held is None else [held])
    rows = 192 * sum(len(members) for members in groups)
    return pl.pallas_call(
        lambda *refs: hidden_kernel(groups, *refs),
        out_shape=jax.ShapeDtypeStruct((64, n, half_width), jnp.bfloat16),
        in_specs=[pl.BlockSpec(memory_space=pltpu.SMEM)] + [vmem] * (len(inputs) - 1),
        out_specs=vmem,
        input_output_aliases={} if held is None else {len(inputs) - 1: 0},
        cost_estimate=pl.CostEstimate(
            flops=2 * rows * 3072 * 1024, bytes_accessed=2 * rows * 3072, transcendentals=rows * 512
        ),
        compiler_params=pltpu.CompilerParams(vmem_limit_bytes=12 * 2**20),
    )(*inputs)


def gather_x(block):
    half = block.shape[0] // 2
    low = lax.ppermute(block, "x", shift("x", 1))
    high = lax.ppermute(block, "x", shift("x", -1))
    low_part, high_part = low[:half], high[half:]
    far_a = lax.ppermute(low_part, "x", shift("x", 1))
    far_b = lax.ppermute(high_part, "x", shift("x", -1))
    return block, low, high, far_a, far_b


def local(tokens, expert_ids, joined_weight):
    zs, copies = lax.axis_size("z"), lax.axis_size("yh")
    yls, xs, cores = lax.axis_size("yl"), lax.axis_size("x"), lax.axis_size("c")
    chips = yls * xs
    part = CAP // cores
    core = lax.axis_index("c")
    here = lax.axis_index("x")
    row = lax.axis_index("yh")
    side = lax.axis_index("yl")
    depth = lax.axis_index("z")
    rows = joined_weight.shape[1]
    chip_width = joined_weight.shape[3] // chips
    half_width = chip_width // cores

    tok_count = tokens.shape[0]
    flat_ids = expert_ids.reshape(-1)
    chosen = (flat_ids[:, None] == jnp.arange(E, dtype=jnp.int32)[None, :]).astype(jnp.int32)
    earlier = jnp.cumsum(chosen, axis=0) - chosen
    position = jnp.sum(earlier * chosen, axis=1)
    slot_index = flat_ids * CAP + position
    slots = jnp.arange(E * CAP, dtype=jnp.int32)
    pick_table = (slot_index[:, None] == slots[None, :]).astype(jnp.bfloat16)

    tok_c = lax.ppermute(tokens, "c", SWAP)
    tok_y = lax.ppermute(tokens, "yl", SWAP)
    tok_yc = lax.ppermute(tokens, ("yl", "c"), [(i, 3 - i) for i in range(4)])
    near = [jnp.where(core == 0, tokens, tok_c), jnp.where(core == 0, tok_c, tokens)]
    far = [jnp.where(core == 0, tok_y, tok_yc), jnp.where(core == 0, tok_yc, tok_y)]
    wide = [jnp.where(side == 0, p, q) for p, q in zip(near + far, far + near)]
    wide = jnp.concatenate(wide, axis=1)

    turn = jnp.arange(zs, dtype=jnp.int32)
    wanted = lax.rem(depth + turn, zs)[:, None] * CAP + core * part
    wanted = (wanted + jnp.arange(part, dtype=jnp.int32)[None, :]).reshape(-1)
    pairs = slot_index.reshape(tok_count, TOP)
    table = (pairs[:, :, None] == wanted[None, None, :]).any(axis=1).astype(jnp.bfloat16)
    placed = lax.dot_general(
        table, wide, (((0,), (0,)), ((), ())), preferred_element_type=jnp.float32
    ).astype(jnp.bfloat16)
    placed = placed.reshape(zs, part, wide.shape[1])
    moved = [placed[0]] + [
        lax.ppermute(placed[s], "z", shift("z", s)) for s in range(1, zs)
    ]
    own = jnp.concatenate(moved, axis=0)
    sources = [own] + [lax.ppermute(own, "yh", shift("yh", s)) for s in range(1, copies)]

    pieces = split_columns(joined_weight, chips * cores)
    w_own = lax.all_to_all(pieces, TENSOR, 0, 0, tiled=True)
    w_own = w_own.reshape(chips * cores * rows, 2 * half_width)
    w_other = lax.ppermute(w_own, "c", SWAP)
    place = jnp.concatenate(
        [
            lax.rem(here + xs + jnp.array([0, -1, 1, 2], jnp.int32), xs),
            jnp.stack([core, 1 - core]),
            lax.rem(row + copies - jnp.arange(copies, dtype=jnp.int32), copies),
            lax.rem(depth + zs - turn, zs),
        ]
    )
    gathered = []
    for members in GROUPS:
        block = jnp.concatenate([sources[m] for m in members], axis=0)
        gathered.append(gather_x(block))
    outgoing = hidden_blocks(
        place, gathered[:2], w_own, w_other, GROUPS[:2], part, half_width
    )
    outgoing = hidden_blocks(
        place, gathered[2:], w_own, w_other, GROUPS[2:], part, half_width, outgoing
    )
    pick_table, outgoing = lax.optimization_barrier((pick_table, outgoing))
    returned = lax.all_to_all(outgoing, ("yh", "z", "c"), 0, 0, tiled=True)
    grouped = returned.reshape(copies, E * CAP, half_width).transpose(1, 0, 2)
    grouped = grouped.reshape(E * CAP, copies * half_width)
    hidden = jnp.dot(pick_table, grouped, preferred_element_type=jnp.float32).astype(jnp.bfloat16)
    return hidden.reshape(tok_count, TOP, copies, half_width)


def solution(mesh):
    fine = Mesh(mesh.devices.reshape(8, 4, 2, 4, 2), ("z", "yh", "yl", "x", "c"))

    return jax.shard_map(
        local,
        mesh=fine,
        in_specs=(P(EXPERT, TENSOR), P(EXPERT, None), P(EXPERT, TENSOR, None, None)),
        out_specs=P(EXPERT, None, None, TENSOR),
        check_vma=False,
    )
```

time: 301 us -> 238 us (0.79)
  the two profiles are of different devices: /device:TPU:10 before, /device:TPU:9 now
where the time goes in v1:
time: 238 us; the launch traced here: 237 us
  starting transfers between devices  112 us (47%)
  blocking collectives  43.3 us (18%)
  waiting for transfers between devices  42.6 us (18%)
  local copies, waits for them, and re-layouts  21.1 us (9%)
  Pallas kernels  15.1 us (6%)
    all_to_all x1, blocking collectives, local(): returned = lax.all_to_all(outgoing, ('yh', 'z', 'c'), 0, 0, tiled=True)  43.3 us
    all_to_all x1, waiting for transfers between devices, local(): w_own = lax.all_to_all(pieces, TENSOR, 0, 0, tiled=True)  28.6 us
    ppermute x7, starting transfers between devices, local(): lax.ppermute(placed[s], 'z', shift('z', s))  28 us
    ppermute x3, starting transfers between devices, gather_x(): high = lax.ppermute(block, 'x', shift('x', -1))  18.9 us
    ppermute x3, starting transfers between devices, gather_x(): far_b = lax.ppermute(high_part, 'x', shift('x', -1))  13.7 us
    ppermute x3, starting transfers between devices, local(): lax.ppermute(own, 'yh', shift('yh', s))  13.5 us
    ppermute x3, waiting for transfers between devices, local(): lax.ppermute(own, 'yh', shift('yh', s))  13.1 us
    pallas_call x2, Pallas kernels, hidden_blocks(): pl.pallas_call(lambda *refs: hidden_kernel(groups, *refs), out_shape=jax....  11.7 us
  transfers between devices with their start and end apart: 27, of which 5 were waited for; matrix products, arithmetic and copies ran while one was open for 8% of the time, Pallas kernels for 3%

profile of v1, /device:TPU:9, one launch (start us, length us, event | category | flops | bytes accessed | tf_op | source)
XLA Modules:
  0.0 237.2 jit_solution(17287357892737228860)
XLA Ops:
  0.0 1.9 copy-done
  1.9 3.4 %shard_map.46 = bf16[16,192,2,256]{3,2,1,0:T(2,128)(2,1)} custom-call(bf16[1,192,2,4096]{3,2,1,0:T(2,128)(2,1)S(1)} %copy-done), custom_call_target="tpu_custom_call" | custom-call | flops 1000000000 | bytes 6291456 | tf_op jit(solution)/shard_map/pallas_call | solution.py:41
  5.4 9.8 %all-to-all-start = ((bf16[16,192,2,256]{3,2,1,0:T(2,128)(2,1)}), bf16[16,192,2,256]{3,2,1,0:T(2,128)(2,1)S(1)}, u32[]{:S(2)}, u32[]{:S(2)}) async-start(bf16[16,192,2,256]{3,2,1,0:T(2,128)(2,1)} %shard_map.46), calls=%async_computation | async-start | bytes 6291456 | tf_op jit(solution)/shard_map/all_to_all | solution.py:163
  15.2 2.3 collective-permute-start.1
  17.5 1.9 collective-permute-start.2
  19.4 3.6 %collective-permute-start.3 = (bf16[128,192]{0,1:T(8,128)(2,1)S(1)}, bf16[128,192]{0,1:T(8,128)(2,1)S(1)}, u32[]{:S(2)}, u32[]{:S(2)}) collective-permute-start(bf16[128,192]{0,1:T(8,128)(2,1)S(1)} %copy-done.3), channel_id=1, source_target_pairs={{0,9},{1,8},{8,1},{9,0},{2,11},{3,10},{10,3},{11,2},{4,13},{5,12},... | collective-permute-start | bytes 147464 | tf_op jit(solution)/shard_map/ppermute | solution.py:141
  24.9 28.6 %all-to-all-done = bf16[16,192,2,256]{3,2,1,0:T(2,128)(2,1)S(1)} async-done(((bf16[16,192,2,256]{3,2,1,0:T(2,128)(2,1)}), bf16[16,192,2,256]{3,2,1,0:T(2,128)(2,1)S(1)}, u32[]{:S(2)}, u32[]{:S(2)}) %all-to-all-start) | async-done | bytes 3145760 | tf_op jit(solution)/shard_map/all_to_all | solution.py:163
  53.6 1.6 copy-done.1
  55.2 2.4 %copy.22 = bf16[384,8,2,256]{3,1,2,0:T(8,128)(2,1)S(1)} copy(bf16[384,8,2,256]{3,2,1,0:T(2,128)(2,1)} %bitcast.23) | data formatting | bytes 6291456
  57.7 3.4 %collective-permute-start = (bf16[3072,512]{1,0:T(8,128)(2,1)S(1)}, bf16[3072,512]{1,0:T(8,128)(2,1)}, u32[]{:S(2)}, u32[]{:S(2)}) collective-permute-start(bf16[3072,512]{1,0:T(8,128)(2,1)S(1)} %bitcast.20), channel_id=1, source_target_pairs={{0,1},{1,0},{2,3},{3,2},{4,5},{5,4},{6,7},{7,6},{8,9},{9,8},{10,11... | collective-permute-start | bytes 9437192 | tf_op jit(solution)/shard_map/ppermute | solution.py:165
  61.4 0.6 fusion.18
  62.1 1.9 collective-permute-start.4
  64.0 4.3 %collective-permute-start.5 = (bf16[24,768]{1,0:T(8,128)(2,1)S(1)}, bf16[24,768]{1,0:T(8,128)(2,1)S(1)}, u32[]{:S(2)}, u32[]{:S(2)}) collective-permute-start(bf16[24,768]{1,0:T(8,128)(2,1)S(1)} %get-tuple-element.14), channel_id=1, source_target_pairs={{0,128},{64,192},{128,256},{192,320},{256,384},{320,448},{384,0},{... | collective-permute-start | bytes 110600 | tf_op jit(solution)/shard_map/ppermute | solution.py:157
  68.3 7.0 %collective-permute-start.6 = (bf16[24,768]{1,0:T(8,128)(2,1)S(1)}, bf16[24,768]{1,0:T(8,128)(2,1)S(1)}, u32[]{:S(2)}, u32[]{:S(2)}) collective-permute-start(bf16[24,768]{1,0:T(8,128)(2,1)S(1)} %get-tuple-element.13), channel_id=1, source_target_pairs={{0,192},{64,256},{128,320},{192,384},{256,448},{320,0},{384,64},{4... | collective-permute-start | bytes 110600 | tf_op jit(solution)/shard_map/ppermute | solution.py:157
  75.4 2.8 %collective-permute-start.7 = (bf16[24,768]{1,0:T(8,128)(2,1)S(1)}, bf16[24,768]{1,0:T(8,128)(2,1)S(1)}, u32[]{:S(2)}, u32[]{:S(2)}) collective-permute-start(bf16[24,768]{1,0:T(8,128)(2,1)S(1)} %get-tuple-element.12), channel_id=1, source_target_pairs={{0,256},{64,320},{128,384},{192,448},{256,0},{320,64},{384,128},{4... | collective-permute-start | bytes 110600 | tf_op jit(solution)/shard_map/ppermute | solution.py:157
  78.2 6.4 %collective-permute-start.8 = (bf16[24,768]{1,0:T(8,128)(2,1)S(1)}, bf16[24,768]{1,0:T(8,128)(2,1)S(1)}, u32[]{:S(2)}, u32[]{:S(2)}) collective-permute-start(bf16[24,768]{1,0:T(8,128)(2,1)S(1)} %get-tuple-element.11), channel_id=1, source_target_pairs={{0,320},{64,384},{128,448},{192,0},{256,64},{320,128},{384,192},{4... | collective-permute-start | bytes 110600 | tf_op jit(solution)/shard_map/ppermute | solution.py:157
  85.2 3.4 %collective-permute-start.9 = (bf16[24,768]{1,0:T(8,128)(2,1)S(1)}, bf16[24,768]{1,0:T(8,128)(2,1)S(1)}, u32[]{:S(2)}, u32[]{:S(2)}) collective-permute-start(bf16[24,768]{1,0:T(8,128)(2,1)S(1)} %get-tuple-element.10), channel_id=1, source_target_pairs={{0,384},{64,448},{128,0},{192,64},{256,128},{320,192},{384,256},{4... | collective-permute-start | bytes 110600 | tf_op jit(solution)/shard_map/ppermute | solution.py:157
  89.2 2.2 collective-permute-start.10
  94.5 4.2 %collective-permute-start.20 = (bf16[192,768]{1,0:T(8,128)(2,1)}, bf16[192,768]{1,0:T(8,128)(2,1)S(1)}, u32[]{:S(2)}, u32[]{:S(2)}) collective-permute-start(bf16[192,768]{1,0:T(8,128)(2,1)} %constant_dynamic-update-slice_fusion.refs_3_), channel_id=1, source_target_pairs={{0,16},{16,32},{32,48},{48,0},{1,17},{17,33},{33,49},{49,1},{2,18}... | collective-permute-start | bytes 884744 | tf_op jit(solution)/shard_map/ppermute | solution.py:160
  98.7 3.2 %collective-permute-start.21 = (bf16[192,768]{1,0:T(8,128)(2,1)}, bf16[192,768]{1,0:T(8,128)(2,1)S(1)}, u32[]{:S(2)}, u32[]{:S(2)}) collective-permute-start(bf16[192,768]{1,0:T(8,128)(2,1)} %constant_dynamic-update-slice_fusion.refs_3_), channel_id=1, source_target_pairs={{0,48},{16,0},{32,16},{48,32},{1,49},{17,1},{33,17},{49,33},{2,50}... | collective-permute-start | bytes 884744 | tf_op jit(solution)/shard_map/ppermute | solution.py:160
  101.9 5.0 %collective-permute-done.20 = bf16[192,768]{1,0:T(8,128)(2,1)S(1)} collective-permute-done((bf16[192,768]{1,0:T(8,128)(2,1)}, bf16[192,768]{1,0:T(8,128)(2,1)S(1)}, u32[]{:S(2)}, u32[]{:S(2)}) %collective-permute-start.20) | collective-permute-done | bytes 294944 | tf_op jit(solution)/shard_map/ppermute | solution.py:160
  106.9 0.7 constant_dynamic-update-slice_fusion.8
  107.9 0.7 constant_dynamic-update-slice_fusion.7.refs_8_
  108.7 7.3 %collective-permute-start.22 = (bf16[384,768]{1,0:T(8,128)(2,1)}, bf16[384,768]{1,0:T(8,128)(2,1)}, u32[]{:S(2)}, u32[]{:S(2)}) collective-permute-start(bf16[384,768]{1,0:T(8,128)(2,1)} %constant_dynamic-update-slice_fusion.7.refs_8_), channel_id=1, source_target_pairs={{0,2},{2,4},{4,6},{6,0},{1,3},{3,5},{5,7},{7,1},{8,10},{10,12},{12... | collective-permute-start | bytes 1769480 | tf_op jit(solution)/shard_map/ppermute | solution.py:108
  115.9 10.9 %collective-permute-start.23 = (bf16[384,768]{1,0:T(8,128)(2,1)}, bf16[384,768]{1,0:T(8,128)(2,1)}, u32[]{:S(2)}, u32[]{:S(2)}) collective-permute-start(bf16[384,768]{1,0:T(8,128)(2,1)} %constant_dynamic-update-slice_fusion.7.refs_8_), channel_id=1, source_target_pairs={{0,6},{2,0},{4,2},{6,4},{1,7},{3,1},{5,3},{7,5},{8,14},{10,8},{12,... | collective-permute-start | bytes 1769480 | tf_op jit(solution)/shard_map/ppermute | solution.py:109
  126.9 6.1 %collective-permute-start.11 = (bf16[192,768]{1,0:T(8,128)(2,1)}, bf16[192,768]{1,0:T(8,128)(2,1)}, u32[]{:S(2)}, u32[]{:S(2)}) collective-permute-start(bf16[192,768]{1,0:T(8,128)(2,1)} %constant_dynamic-update-slice_fusion.refs_3_), channel_id=1, source_target_pairs={{0,32},{16,48},{32,0},{48,16},{1,33},{17,49},{33,1},{49,17},{2,34}... | collective-permute-start | bytes 884744 | tf_op jit(solution)/shard_map/ppermute | solution.py:160
  133.0 1.9 collective-permute-start.16
  134.9 7.8 %collective-permute-done.11.refs_3_ = bf16[192,768]{1,0:T(8,128)(2,1)} collective-permute-done((bf16[192,768]{1,0:T(8,128)(2,1)}, bf16[192,768]{1,0:T(8,128)(2,1)}, u32[]{:S(2)}, u32[]{:S(2)}) %collective-permute-start.11) | collective-permute-done | bytes 294944 | tf_op jit(solution)/shard_map/ppermute | solution.py:160
  142.7 3.4 %collective-permute-start.17 = (bf16[192,768]{1,0:T(8,128)(2,1)}, bf16[192,768]{1,0:T(8,128)(2,1)}, u32[]{:S(2)}, u32[]{:S(2)}) collective-permute-start(bf16[192,768]{1,0:T(8,128)(2,1)} %constant_dynamic-update-slice_fusion.refs_3_), channel_id=1, source_target_pairs={{0,6},{2,0},{4,2},{6,4},{1,7},{3,1},{5,3},{7,5},{8,14},{10,8},{12,... | collective-permute-start | bytes 884744 | tf_op jit(solution)/shard_map/ppermute | solution.py:109
  146.1 1.9 collective-permute-start.12
  148.1 4.6 %collective-permute-start.13 = (bf16[192,768]{1,0:T(8,128)(2,1)}, bf16[192,768]{1,0:T(8,128)(2,1)}, u32[]{:S(2)}, u32[]{:S(2)}) collective-permute-start(bf16[192,768]{1,0:T(8,128)(2,1)} %collective-permute-done.11.refs_3_), channel_id=1, source_target_pairs={{0,6},{2,0},{4,2},{6,4},{1,7},{3,1},{5,3},{7,5},{8,14},{10,8},{12,... | collective-permute-start | bytes 884744 | tf_op jit(solution)/shard_map/ppermute | solution.py:109
  152.7 1.7 slice.85
  154.4 1.7 slice.86
  156.1 1.9 collective-permute-start.24
  158.0 4.6 %collective-permute-start.25 = (bf16[192,768]{1,0:T(8,128)(2,1)}, bf16[192,768]{1,0:T(8,128)(2,1)}, u32[]{:S(2)}, u32[]{:S(2)}) collective-permute-start(bf16[192,768]{1,0:T(8,128)(2,1)} %slice.86), channel_id=1, source_target_pairs={{0,6},{2,0},{4,2},{6,4},{1,7},{3,1},{5,3},{7,5},{8,14},{10,8},{12,... | collective-permute-start | bytes 884744 | tf_op jit(solution)/shard_map/ppermute | solution.py:112
  162.7 0.9 slice.83
  163.6 0.9 slice.84
  164.6 1.9 collective-permute-start.18
  166.5 4.6 %collective-permute-start.19 = (bf16[96,768]{1,0:T(8,128)(2,1)S(1)}, bf16[96,768]{1,0:T(8,128)(2,1)S(1)}, u32[]{:S(2)}, u32[]{:S(2)}) collective-permute-start(bf16[96,768]{1,0:T(8,128)(2,1)S(1)} %slice.84), channel_id=1, source_target_pairs={{0,6},{2,0},{4,2},{6,4},{1,7},{3,1},{5,3},{7,5},{8,14},{10,8},{12,... | collective-permute-start | bytes 442376 | tf_op jit(solution)/shard_map/ppermute | solution.py:112
  171.1 0.8 fusion
  171.9 0.9 slice.82
  172.8 0.8 collective-permute-done.18.refs_6_
  173.6 1.9 collective-permute-start.14
  175.6 4.6 %collective-permute-start.15 = (bf16[96,768]{1,0:T(8,128)(2,1)S(1)}, bf16[96,768]{1,0:T(8,128)(2,1)S(1)}, u32[]{:S(2)}, u32[]{:S(2)}) collective-permute-start(bf16[96,768]{1,0:T(8,128)(2,1)S(1)} %slice.82), channel_id=1, source_target_pairs={{0,6},{2,0},{4,2},{6,4},{1,7},{3,1},{5,3},{7,5},{8,14},{10,8},{12,... | collective-permute-start | bytes 442376 | tf_op jit(solution)/shard_map/ppermute | solution.py:112
  180.2 7.8 %shard_map.47.refs_8_ = bf16[64,24,256]{2,1,0:T(8,128)(2,1)S(1)} custom-call(s32[18]{0:T(128)S(1)} %concatenate.12.refs_0_, bf16[3072,512]{1,0:T(8,128)(2,1)S(1)} %bitcast.21, bf16[3072,512]{1,0:T(8,128)(2,1)} %collective-permute-done.refs_2_, bf16[192,768]{1,0:T(8,128)(2,1)} %constant_dynamic-update-slice_fusion.refs_3_, ...), custom_call_target="tpu_custom_call" | custom-call | flops 3623878656 | bytes 3538944 | tf_op jit(solution)/shard_map/pallas_call | solution.py:93
  188.0 3.8 %shard_map.48 = bf16[64,24,256]{2,1,0:T(8,128)(2,1)S(1)} custom-call(s32[18]{0:T(128)S(1)} %concatenate.12.refs_0_, bf16[3072,512]{1,0:T(8,128)(2,1)S(1)} %bitcast.22, bf16[3072,512]{1,0:T(8,128)(2,1)} %collective-permute-done.refs_2_, bf16[192,768]{1,0:T(8,128)(2,1)} %collective-permute-done.11.refs_3_, ...), custom_call_target="tpu_custom_call", output_to_operand_aliasing={{}: (8, {})} | custom-call | flops 1207959552 | bytes 1179648 | tf_op jit(solution)/shard_map/pallas_call | solution.py:93
  191.9 43.3 %all_to_all.10 = bf16[64,24,256]{2,1,0:T(8,128)(2,1)S(1)} all-to-all(bf16[64,24,256]{2,1,0:T(8,128)(2,1)S(1)} %shard_map.48), channel_id=1, replica_groups=mesh['z'=8,'yh'=4,'yl'=2,'x'=4,'c'=2] {'yh','z','c'}, dimensions={0} | all-to-all | bytes 1572864 | tf_op jit(solution)/shard_map/all_to_all | solution.py:185
  236.0 1.2 reshape.96
  (65 shorter events, 7.7 us)
Async XLA Ops:
  0.0 1.9 copy-start
  5.3 9.8 %copy-start.3 = (bf16[128,192]{0,1:T(8,128)(2,1)S(1)}, bf16[128,192]{0,1:T(8,128)(2,1)}, u32[]{:S(2)}) copy-start(bf16[128,192]{0,1:T(8,128)(2,1)} %param.4) | copy-start | bytes 147460
  5.3 17.7 %copy-start.4 = (s32[128,2]{0,1:T(2,128)S(1)}, s32[128,2]{0,1:T(2,128)}, u32[]{:S(2)}) copy-start(s32[128,2]{0,1:T(2,128)} %param.5) | copy-start | bytes 3076
  5.4 48.2 %all-to-all-start = ((bf16[16,192,2,256]{3,2,1,0:T(2,128)(2,1)}), bf16[16,192,2,256]{3,2,1,0:T(2,128)(2,1)S(1)}, u32[]{:S(2)}, u32[]{:S(2)}) async-start(bf16[16,192,2,256]{3,2,1,0:T(2,128)(2,1)} %shard_map.46), calls=%async_computation | async-start | bytes 6291456 | tf_op jit(solution)/shard_map/all_to_all | solution.py:163
  15.2 45.9 %collective-permute-start.1 = (bf16[128,192]{0,1:T(8,128)(2,1)S(1)}, bf16[128,192]{0,1:T(8,128)(2,1)S(1)}, u32[]{:S(2)}, u32[]{:S(2)}) collective-permute-start(bf16[128,192]{0,1:T(8,128)(2,1)S(1)} %copy-done.3), channel_id=1, source_target_pairs={{0,1},{1,0},{2,3},{3,2},{4,5},{5,4},{6,7},{7,6},{8,9},{9,8},{10,11... | collective-permute-start | bytes 147464 | tf_op jit(solution)/shard_map/ppermute | solution.py:139
  17.5 43.6 %collective-permute-start.2 = (bf16[128,192]{0,1:T(8,128)(2,1)S(1)}, bf16[128,192]{0,1:T(8,128)(2,1)S(1)}, u32[]{:S(2)}, u32[]{:S(2)}) collective-permute-start(bf16[128,192]{0,1:T(8,128)(2,1)S(1)} %copy-done.3), channel_id=1, source_target_pairs={{0,8},{8,0},{1,9},{9,1},{2,10},{10,2},{3,11},{11,3},{4,12},{12,4},... | collective-permute-start | bytes 147464 | tf_op jit(solution)/shard_map/ppermute | solution.py:140
  19.4 41.7 %collective-permute-start.3 = (bf16[128,192]{0,1:T(8,128)(2,1)S(1)}, bf16[128,192]{0,1:T(8,128)(2,1)S(1)}, u32[]{:S(2)}, u32[]{:S(2)}) collective-permute-start(bf16[128,192]{0,1:T(8,128)(2,1)S(1)} %copy-done.3), channel_id=1, source_target_pairs={{0,9},{1,8},{8,1},{9,0},{2,11},{3,10},{10,3},{11,2},{4,13},{5,12},... | collective-permute-start | bytes 147464 | tf_op jit(solution)/shard_map/ppermute | solution.py:141
  53.6 1.6 copy-start.1
  57.6 95.0 %copy-start.5 = (s32[4]{0:T(128)S(1)}, s32[4]{0:T(128)}, u32[]{:S(2)}) copy-start(s32[4]{0:T(128)} %constant.53.clone) | copy-start | bytes 52
  57.7 122.5 %collective-permute-start = (bf16[3072,512]{1,0:T(8,128)(2,1)S(1)}, bf16[3072,512]{1,0:T(8,128)(2,1)}, u32[]{:S(2)}, u32[]{:S(2)}) collective-permute-start(bf16[3072,512]{1,0:T(8,128)(2,1)S(1)} %bitcast.20), channel_id=1, source_target_pairs={{0,1},{1,0},{2,3},{3,2},{4,5},{5,4},{6,7},{7,6},{8,9},{9,8},{10,11... | collective-permute-start | bytes 9437192 | tf_op jit(solution)/shard_map/ppermute | solution.py:165
  62.1 16.1 %collective-permute-start.4 = (bf16[24,768]{1,0:T(8,128)(2,1)S(1)}, bf16[24,768]{1,0:T(8,128)(2,1)S(1)}, u32[]{:S(2)}, u32[]{:S(2)}) collective-permute-start(bf16[24,768]{1,0:T(8,128)(2,1)S(1)} %get-tuple-element.15), channel_id=1, source_target_pairs={{0,64},{64,128},{128,192},{192,256},{256,320},{320,384},{384,448},... | collective-permute-start | bytes 110600 | tf_op jit(solution)/shard_map/ppermute | solution.py:157
  64.0 21.2 %collective-permute-start.5 = (bf16[24,768]{1,0:T(8,128)(2,1)S(1)}, bf16[24,768]{1,0:T(8,128)(2,1)S(1)}, u32[]{:S(2)}, u32[]{:S(2)}) collective-permute-start(bf16[24,768]{1,0:T(8,128)(2,1)S(1)} %get-tuple-element.14), channel_id=1, source_target_pairs={{0,128},{64,192},{128,256},{192,320},{256,384},{320,448},{384,0},{... | collective-permute-start | bytes 110600 | tf_op jit(solution)/shard_map/ppermute | solution.py:157
  68.3 20.9 %collective-permute-start.6 = (bf16[24,768]{1,0:T(8,128)(2,1)S(1)}, bf16[24,768]{1,0:T(8,128)(2,1)S(1)}, u32[]{:S(2)}, u32[]{:S(2)}) collective-permute-start(bf16[24,768]{1,0:T(8,128)(2,1)S(1)} %get-tuple-element.13), channel_id=1, source_target_pairs={{0,192},{64,256},{128,320},{192,384},{256,448},{320,0},{384,64},{4... | collective-permute-start | bytes 110600 | tf_op jit(solution)/shard_map/ppermute | solution.py:157
  75.4 16.7 %collective-permute-start.7 = (bf16[24,768]{1,0:T(8,128)(2,1)S(1)}, bf16[24,768]{1,0:T(8,128)(2,1)S(1)}, u32[]{:S(2)}, u32[]{:S(2)}) collective-permute-start(bf16[24,768]{1,0:T(8,128)(2,1)S(1)} %get-tuple-element.12), channel_id=1, source_target_pairs={{0,256},{64,320},{128,384},{192,448},{256,0},{320,64},{384,128},{4... | collective-permute-start | bytes 110600 | tf_op jit(solution)/shard_map/ppermute | solution.py:157
  78.2 14.4 %collective-permute-start.8 = (bf16[24,768]{1,0:T(8,128)(2,1)S(1)}, bf16[24,768]{1,0:T(8,128)(2,1)S(1)}, u32[]{:S(2)}, u32[]{:S(2)}) collective-permute-start(bf16[24,768]{1,0:T(8,128)(2,1)S(1)} %get-tuple-element.11), channel_id=1, source_target_pairs={{0,320},{64,384},{128,448},{192,0},{256,64},{320,128},{384,192},{4... | collective-permute-start | bytes 110600 | tf_op jit(solution)/shard_map/ppermute | solution.py:157
  85.2 8.1 %collective-permute-start.9 = (bf16[24,768]{1,0:T(8,128)(2,1)S(1)}, bf16[24,768]{1,0:T(8,128)(2,1)S(1)}, u32[]{:S(2)}, u32[]{:S(2)}) collective-permute-start(bf16[24,768]{1,0:T(8,128)(2,1)S(1)} %get-tuple-element.10), channel_id=1, source_target_pairs={{0,384},{64,448},{128,0},{192,64},{256,128},{320,192},{384,256},{4... | collective-permute-start | bytes 110600 | tf_op jit(solution)/shard_map/ppermute | solution.py:157
  89.2 4.7 %collective-permute-start.10 = (bf16[24,768]{1,0:T(8,128)(2,1)S(1)}, bf16[24,768]{1,0:T(8,128)(2,1)S(1)}, u32[]{:S(2)}, u32[]{:S(2)}) collective-permute-start(bf16[24,768]{1,0:T(8,128)(2,1)S(1)} %get-tuple-element.9), channel_id=1, source_target_pairs={{0,448},{64,0},{128,64},{192,128},{256,192},{320,256},{384,320},{4... | collective-permute-start | bytes 110600 | tf_op jit(solution)/shard_map/ppermute | solution.py:157
  94.5 12.4 %collective-permute-start.20 = (bf16[192,768]{1,0:T(8,128)(2,1)}, bf16[192,768]{1,0:T(8,128)(2,1)S(1)}, u32[]{:S(2)}, u32[]{:S(2)}) collective-permute-start(bf16[192,768]{1,0:T(8,128)(2,1)} %constant_dynamic-update-slice_fusion.refs_3_), channel_id=1, source_target_pairs={{0,16},{16,32},{32,48},{48,0},{1,17},{17,33},{33,49},{49,1},{2,18}... | collective-permute-start | bytes 884744 | tf_op jit(solution)/shard_map/ppermute | solution.py:160
  98.7 9.2 %collective-permute-start.21 = (bf16[192,768]{1,0:T(8,128)(2,1)}, bf16[192,768]{1,0:T(8,128)(2,1)S(1)}, u32[]{:S(2)}, u32[]{:S(2)}) collective-permute-start(bf16[192,768]{1,0:T(8,128)(2,1)} %constant_dynamic-update-slice_fusion.refs_3_), channel_id=1, source_target_pairs={{0,48},{16,0},{32,16},{48,32},{1,49},{17,1},{33,17},{49,33},{2,50}... | collective-permute-start | bytes 884744 | tf_op jit(solution)/shard_map/ppermute | solution.py:160
  108.7 37.5 %collective-permute-start.22 = (bf16[384,768]{1,0:T(8,128)(2,1)}, bf16[384,768]{1,0:T(8,128)(2,1)}, u32[]{:S(2)}, u32[]{:S(2)}) collective-permute-start(bf16[384,768]{1,0:T(8,128)(2,1)} %constant_dynamic-update-slice_fusion.7.refs_8_), channel_id=1, source_target_pairs={{0,2},{2,4},{4,6},{6,0},{1,3},{3,5},{5,7},{7,1},{8,10},{10,12},{12... | collective-permute-start | bytes 1769480 | tf_op jit(solution)/shard_map/ppermute | solution.py:108
  115.9 32.1 %collective-permute-start.23 = (bf16[384,768]{1,0:T(8,128)(2,1)}, bf16[384,768]{1,0:T(8,128)(2,1)}, u32[]{:S(2)}, u32[]{:S(2)}) collective-permute-start(bf16[384,768]{1,0:T(8,128)(2,1)} %constant_dynamic-update-slice_fusion.7.refs_8_), channel_id=1, source_target_pairs={{0,6},{2,0},{4,2},{6,4},{1,7},{3,1},{5,3},{7,5},{8,14},{10,8},{12,... | collective-permute-start | bytes 1769480 | tf_op jit(solution)/shard_map/ppermute | solution.py:109
  126.9 15.9 %collective-permute-start.11 = (bf16[192,768]{1,0:T(8,128)(2,1)}, bf16[192,768]{1,0:T(8,128)(2,1)}, u32[]{:S(2)}, u32[]{:S(2)}) collective-permute-start(bf16[192,768]{1,0:T(8,128)(2,1)} %constant_dynamic-update-slice_fusion.refs_3_), channel_id=1, source_target_pairs={{0,32},{16,48},{32,0},{48,16},{1,33},{17,49},{33,1},{49,17},{2,34}... | collective-permute-start | bytes 884744 | tf_op jit(solution)/shard_map/ppermute | solution.py:160
  133.0 23.1 %collective-permute-start.16 = (bf16[192,768]{1,0:T(8,128)(2,1)}, bf16[192,768]{1,0:T(8,128)(2,1)}, u32[]{:S(2)}, u32[]{:S(2)}) collective-permute-start(bf16[192,768]{1,0:T(8,128)(2,1)} %constant_dynamic-update-slice_fusion.refs_3_), channel_id=1, source_target_pairs={{0,2},{2,4},{4,6},{6,0},{1,3},{3,5},{5,7},{7,1},{8,10},{10,12},{12... | collective-permute-start | bytes 884744 | tf_op jit(solution)/shard_map/ppermute | solution.py:108
  142.7 15.2 %collective-permute-start.17 = (bf16[192,768]{1,0:T(8,128)(2,1)}, bf16[192,768]{1,0:T(8,128)(2,1)}, u32[]{:S(2)}, u32[]{:S(2)}) collective-permute-start(bf16[192,768]{1,0:T(8,128)(2,1)} %constant_dynamic-update-slice_fusion.refs_3_), channel_id=1, source_target_pairs={{0,6},{2,0},{4,2},{6,4},{1,7},{3,1},{5,3},{7,5},{8,14},{10,8},{12,... | collective-permute-start | bytes 884744 | tf_op jit(solution)/shard_map/ppermute | solution.py:109
  146.1 18.4 %collective-permute-start.12 = (bf16[192,768]{1,0:T(8,128)(2,1)}, bf16[192,768]{1,0:T(8,128)(2,1)S(1)}, u32[]{:S(2)}, u32[]{:S(2)}) collective-permute-start(bf16[192,768]{1,0:T(8,128)(2,1)} %collective-permute-done.11.refs_3_), channel_id=1, source_target_pairs={{0,2},{2,4},{4,6},{6,0},{1,3},{3,5},{5,7},{7,1},{8,10},{10,12},{12... | collective-permute-start | bytes 884744 | tf_op jit(solution)/shard_map/ppermute | solution.py:108
  148.1 18.4 %collective-permute-start.13 = (bf16[192,768]{1,0:T(8,128)(2,1)}, bf16[192,768]{1,0:T(8,128)(2,1)}, u32[]{:S(2)}, u32[]{:S(2)}) collective-permute-start(bf16[192,768]{1,0:T(8,128)(2,1)} %collective-permute-done.11.refs_3_), channel_id=1, source_target_pairs={{0,6},{2,0},{4,2},{6,4},{1,7},{3,1},{5,3},{7,5},{8,14},{10,8},{12,... | collective-permute-start | bytes 884744 | tf_op jit(solution)/shard_map/ppermute | solution.py:109
  156.1 24.1 %collective-permute-start.24 = (bf16[192,768]{1,0:T(8,128)(2,1)}, bf16[192,768]{1,0:T(8,128)(2,1)}, u32[]{:S(2)}, u32[]{:S(2)}) collective-permute-start(bf16[192,768]{1,0:T(8,128)(2,1)} %slice.85), channel_id=1, source_target_pairs={{0,2},{2,4},{4,6},{6,0},{1,3},{3,5},{5,7},{7,1},{8,10},{10,12},{12... | collective-permute-start | bytes 884744 | tf_op jit(solution)/shard_map/ppermute | solution.py:111
  158.0 22.1 %collective-permute-start.25 = (bf16[192,768]{1,0:T(8,128)(2,1)}, bf16[192,768]{1,0:T(8,128)(2,1)}, u32[]{:S(2)}, u32[]{:S(2)}) collective-permute-start(bf16[192,768]{1,0:T(8,128)(2,1)} %slice.86), channel_id=1, source_target_pairs={{0,6},{2,0},{4,2},{6,4},{1,7},{3,1},{5,3},{7,5},{8,14},{10,8},{12,... | collective-permute-start | bytes 884744 | tf_op jit(solution)/shard_map/ppermute | solution.py:112
  164.6 9.1 %collective-permute-start.18 = (bf16[96,768]{1,0:T(8,128)(2,1)S(1)}, bf16[96,768]{1,0:T(8,128)(2,1)S(1)}, u32[]{:S(2)}, u32[]{:S(2)}) collective-permute-start(bf16[96,768]{1,0:T(8,128)(2,1)S(1)} %slice.83), channel_id=1, source_target_pairs={{0,2},{2,4},{4,6},{6,0},{1,3},{3,5},{5,7},{7,1},{8,10},{10,12},{12... | collective-permute-start | bytes 442376 | tf_op jit(solution)/shard_map/ppermute | solution.py:111
  166.5 9.1 %collective-permute-start.19 = (bf16[96,768]{1,0:T(8,128)(2,1)S(1)}, bf16[96,768]{1,0:T(8,128)(2,1)S(1)}, u32[]{:S(2)}, u32[]{:S(2)}) collective-permute-start(bf16[96,768]{1,0:T(8,128)(2,1)S(1)} %slice.84), channel_id=1, source_target_pairs={{0,6},{2,0},{4,2},{6,4},{1,7},{3,1},{5,3},{7,5},{8,14},{10,8},{12,... | collective-permute-start | bytes 442376 | tf_op jit(solution)/shard_map/ppermute | solution.py:112
  173.6 14.4 %collective-permute-start.14 = (bf16[96,768]{1,0:T(8,128)(2,1)S(1)}, bf16[96,768]{1,0:T(8,128)(2,1)S(1)}, u32[]{:S(2)}, u32[]{:S(2)}) collective-permute-start(bf16[96,768]{1,0:T(8,128)(2,1)S(1)} %slice.81), channel_id=1, source_target_pairs={{0,2},{2,4},{4,6},{6,0},{1,3},{3,5},{5,7},{7,1},{8,10},{10,12},{12... | collective-permute-start | bytes 442376 | tf_op jit(solution)/shard_map/ppermute | solution.py:111
  175.6 12.5 %collective-permute-start.15 = (bf16[96,768]{1,0:T(8,128)(2,1)S(1)}, bf16[96,768]{1,0:T(8,128)(2,1)S(1)}, u32[]{:S(2)}, u32[]{:S(2)}) collective-permute-start(bf16[96,768]{1,0:T(8,128)(2,1)S(1)} %slice.82), channel_id=1, source_target_pairs={{0,6},{2,0},{4,2},{6,4},{1,7},{3,1},{5,3},{7,5},{8,14},{10,8},{12,... | collective-permute-start | bytes 442376 | tf_op jit(solution)/shard_map/ppermute | solution.py:112
  191.9 43.7 %copy-start.2 = (bf16[256,384]{1,0:T(8,128)(2,1)S(1)}, bf16[256,384]{1,0:T(8,128)(2,1)}, u32[]{:S(2)}) copy-start(bf16[256,384]{1,0:T(8,128)(2,1)} %fusion) | copy-start | bytes 589828

commit v2 on v0

v2 whole, which is shorter than its diff:
```python
import jax
import jax.numpy as jnp
from jax import lax
from jax.experimental import pallas as pl
from jax.experimental.pallas import tpu as pltpu
from jax.sharding import Mesh, PartitionSpec as P

E = 8
TOP = 2
CAP = 48


EXPERT = ("z", "yh")
TENSOR = ("yl", "x", "c")
CHIPS = ("yl", "x")
SWAP = [(0, 1), (1, 0)]


def shift(axis, by):
    n = lax.axis_size(axis)
    return [(i, (i + by) % n) for i in range(n)]


def chip_shift(side, by):
    return [(i, (i // 4 + side) % 2 * 4 + (i % 4 + by) % 4) for i in range(8)]


def split_kernel(chip, w_ref, *refs):
    *outs, sems = refs
    width = outs[0].shape[2]
    copies = []
    for p, out in enumerate(outs):
        at = pl.multiple_of(chip[p] * width, width)
        copies.append(pltpu.make_async_copy(w_ref.at[0, :, :, pl.ds(at, width)], out, sems.at[p]))
    for copy in copies:
        copy.start()
    for copy in copies:
        copy.wait()


def split_columns(joined_weight, chip):
    _, rows, two, columns = joined_weight.shape
    chips = chip.shape[0]
    piece = jax.ShapeDtypeStruct((rows, two, columns // chips), joined_weight.dtype)
    vmem = pl.BlockSpec(memory_space=pltpu.VMEM)
    return pl.pallas_call(
        split_kernel,
        out_shape=[piece] * chips,
        in_specs=[pl.BlockSpec(memory_space=pltpu.SMEM), pl.BlockSpec(memory_space=pltpu.HBM)],
        out_specs=[vmem] * chips,
        scratch_shapes=[pltpu.SemaphoreType.DMA((chips,))],
        cost_estimate=pl.CostEstimate(flops=10**9, bytes_accessed=2 * 3 * 2**20, transcendentals=0),
        compiler_params=pltpu.CompilerParams(vmem_limit_bytes=8 * 2**20),
    )(chip, joined_weight)


BLOCK = 192


def add_product(total, x, s, w_mine, w_other, columns):
    w = jnp.concatenate([w_mine[s, :, columns], w_other[s, :, columns]], axis=0)
    return total + jnp.dot(x, w, preferred_element_type=jnp.float32)


def near_kernel(w_mine, w_other, *refs):
    *pieces, out = refs
    width = out.shape[1] // 2
    for start in range(0, out.shape[0], BLOCK):
        rows = slice(start, start + BLOCK)
        for side in range(2):
            columns = slice(side * width, (side + 1) * width)
            total = jnp.zeros((BLOCK, width), jnp.float32)
            for x, s in zip(pieces, (0, 1, 3, 4, 5, 7)):
                total = add_product(total, x[rows], s, w_mine, w_other, columns)
            out[rows, columns] = total


def hidden_kernel(w_mine, w_other, low0, high0, low1, high1, sums, out):
    copies, zs, cores = 4, 8, 2
    n, half_width = out.shape[1], out.shape[2]
    width, cut = cores * half_width, low0.shape[0]
    for start in range(0, sums.shape[0], BLOCK):
        rows = slice(start, start + BLOCK)
        if start < cut:
            x0, x1 = low0[rows], low1[rows]
        else:
            x0, x1 = high0[start - cut : start - cut + BLOCK], high1[start - cut : start - cut + BLOCK]
        for c in range(cores):
            both = []
            for first in (c * half_width, width + c * half_width):
                columns = slice(first, first + half_width)
                total = add_product(sums[rows, columns], x0, 2, w_mine, w_other, columns)
                both.append(add_product(total, x1, 6, w_mine, w_other, columns))
            gate, up = both
            active = (gate / (1.0 + jnp.exp(-gate)) * up).astype(jnp.bfloat16)
            for j in range(BLOCK // n):
                z, row = divmod(start // n + j, copies)
                out[(row * zs + z) * cores + c] = active[j * n : (j + 1) * n]


def on_core(kernel, out_shape, *inputs):
    vmem = pl.BlockSpec(memory_space=pltpu.VMEM)
    return pl.pallas_call(
        kernel,
        out_shape=out_shape,
        in_specs=[vmem] * len(inputs),
        out_specs=vmem,
        cost_estimate=pl.CostEstimate(
            flops=768 * 3072 * 1024, bytes_accessed=6 * 2**20, transcendentals=768 * 512
        ),
        compiler_params=pltpu.CompilerParams(vmem_limit_bytes=12 * 2**20),
    )(*inputs)


def gather_x(block):
    half = block.shape[0] // 2
    low = lax.ppermute(block, "x", shift("x", 1))
    high = lax.ppermute(block, "x", shift("x", -1))
    low_part, high_part = low[:half], high[half:]
    far_a = lax.ppermute(low_part, "x", shift("x", 1))
    far_b = lax.ppermute(high_part, "x", shift("x", -1))
    return block, low, high, far_a, far_b


def local(tokens, expert_ids, joined_weight):
    zs, copies = lax.axis_size("z"), lax.axis_size("yh")
    yls, xs, cores = lax.axis_size("yl"), lax.axis_size("x"), lax.axis_size("c")
    chips = yls * xs
    part = CAP // cores
    core, here, side = lax.axis_index("c"), lax.axis_index("x"), lax.axis_index("yl")
    rows = joined_weight.shape[1]
    chip_width = joined_weight.shape[3] // chips
    half_width = chip_width // cores

    tok_count = tokens.shape[0]
    flat_ids = expert_ids.reshape(-1)
    chosen = (flat_ids[:, None] == jnp.arange(E, dtype=jnp.int32)[None, :]).astype(jnp.int32)
    earlier = jnp.cumsum(chosen, axis=0) - chosen
    position = jnp.sum(earlier * chosen, axis=1)
    slot_index = flat_ids * CAP + position
    slots = jnp.arange(E * CAP, dtype=jnp.int32)
    pick_table = (slot_index[:, None] == slots[None, :]).astype(jnp.bfloat16)
    token_table = pick_table.reshape(tok_count, TOP, E * CAP).sum(axis=1)
    placed = lax.dot_general(
        token_table, tokens, (((0,), (0,)), ((), ())), preferred_element_type=jnp.float32
    ).astype(jnp.bfloat16)

    sent = placed.reshape(zs, 1, cores, part, rows)
    sent = jnp.broadcast_to(sent, (zs, copies, cores, part, rows)).reshape(-1, part, rows)
    got = lax.all_to_all(sent, ("z", "yh", "c"), 0, 0, tiled=True)
    got = got.reshape(zs * copies, cores, part, rows)

    turn = jnp.arange(chips, dtype=jnp.int32)
    chip = lax.rem(side + turn // xs, yls) * xs + lax.rem(here + turn % xs, xs)
    pieces = split_columns(joined_weight, chip)
    moved = [pieces[0]]
    for s in range(1, chips):
        moved.append(lax.ppermute(pieces[s], CHIPS, chip_shift(s // xs, s % xs)))
    mine = jnp.where(core == 0, got[:, 0], got[:, 1])
    theirs = jnp.where(core == 0, got[:, 1], got[:, 0])
    own = jnp.concatenate([mine, theirs], axis=-1).reshape(zs * copies * part, cores * rows)
    opposite = lax.ppermute(own, "yl", SWAP)
    moved, opposite = lax.optimization_barrier((moved, opposite))
    w_mine = jnp.concatenate([m.reshape(rows, 2 * chip_width) for m in moved], axis=0)
    w_other = lax.ppermute(w_mine, "c", SWAP)
    shape = (chips, rows, 2 * chip_width)
    w_mine, w_other = w_mine.reshape(shape), w_other.reshape(shape)

    near = gather_x(own)
    far = gather_x(opposite)
    sums = jax.ShapeDtypeStruct((own.shape[0], 2 * chip_width), jnp.float32)
    half_sums = on_core(near_kernel, sums, w_mine, w_other, *near[:3], *far[:3])
    active = jax.ShapeDtypeStruct((zs * copies * cores, part, half_width), jnp.bfloat16)
    outgoing = on_core(hidden_kernel, active, w_mine, w_other, *near[3:], *far[3:], half_sums)

    pick_table, outgoing = lax.optimization_barrier((pick_table, outgoing))
    returned = lax.all_to_all(outgoing, ("yh", "z", "c"), 0, 0, tiled=True)
    grouped = returned.reshape(copies, E * CAP, half_width).transpose(1, 0, 2)
    grouped = grouped.reshape(E * CAP, copies * half_width)
    hidden = jnp.dot(pick_table, grouped, preferred_element_type=jnp.float32).astype(jnp.bfloat16)
    return hidden.reshape(tok_count, TOP, copies, half_width)


def solution(mesh):
    fine = Mesh(mesh.devices.reshape(8, 4, 2, 4, 2), ("z", "yh", "yl", "x", "c"))

    return jax.shard_map(
        local,
        mesh=fine,
        in_specs=(P(EXPERT, TENSOR), P(EXPERT, None), P(EXPERT, TENSOR, None, None)),
        out_specs=P(EXPERT, None, None, TENSOR),
        check_vma=False,
    )
```

time: 301 us -> 190 us (0.63)
  the two profiles are of different devices: /device:TPU:10 before, /device:TPU:1 now
where the time goes in v2:
time: 190 us; the launch traced here: 189 us
  starting transfers between devices  74 us (39%)
  waiting for transfers between devices  61.4 us (32%)
  blocking collectives  31.4 us (17%)
  local copies, waits for them, and re-layouts  9.68 us (5%)
  Pallas kernels  8.32 us (4%)
  other arithmetic  3.04 us (2%)
    ppermute x7, waiting for transfers between devices, local(): moved.append(lax.ppermute(pieces[s], CHIPS, chip_shift(s // xs, s % xs)))  34.4 us
    all_to_all x1, blocking collectives, local(): returned = lax.all_to_all(outgoing, ('yh', 'z', 'c'), 0, 0, tiled=True)  31.4 us
    ppermute x7, starting transfers between devices, local(): moved.append(lax.ppermute(pieces[s], CHIPS, chip_shift(s // xs, s % xs)))  25.1 us
    all_to_all x1, starting transfers between devices, local(): got = lax.all_to_all(sent, ('z', 'yh', 'c'), 0, 0, tiled=True)  17.8 us
    all_to_all x1, waiting for transfers between devices, local(): got = lax.all_to_all(sent, ('z', 'yh', 'c'), 0, 0, tiled=True)  12.8 us
    ppermute x2, waiting for transfers between devices, gather_x(): low = lax.ppermute(block, 'x', shift('x', 1))  11 us
    ppermute x2, starting transfers between devices, gather_x(): far_b = lax.ppermute(high_part, 'x', shift('x', -1))  7.91 us
    pallas_call x2, Pallas kernels, on_core(): pl.pallas_call(kernel, out_shape=out_shape, in_specs=[vmem] * len(inputs)...  6.87 us
  transfers between devices with their start and end apart: 18, of which 9 were waited for; matrix products, arithmetic and copies ran while one was open for 1% of the time, Pallas kernels for 3%

profile of v2, /device:TPU:1, one launch (start us, length us, event | category | flops | bytes accessed | tf_op | source)
XLA Modules:
  0.0 188.9 jit_solution(12181365399204980639)
XLA Ops:
  0.0 0.8 copy.19
  1.1 0.6 reduce-window.6
  1.7 0.2 slice_reduce_fusion
  2.0 0.1 reduce_sum.24
  2.2 0.7 multiply_add_fusion
  3.1 0.2 convolution_convert_fusion.1
  3.3 0.1 copy.22
  3.4 1.0 broadcast_in_dim.5
  4.4 17.8 %all-to-all-start = ((bf16[64,24,192]{2,1,0:T(8,128)(2,1)}), bf16[64,24,192]{2,1,0:T(8,128)(2,1)}, u32[]{:S(2)}, u32[]{:S(2)}) async-start(bf16[64,24,192]{2,1,0:T(8,128)(2,1)} %bitcast.3), calls=%async_computation | async-start | bytes 1572864 | tf_op jit(solution)/shard_map/all_to_all | solution.py:150
  22.2 1.9 copy-done.1
  24.1 1.5 shard_map.37
  25.5 3.1 %collective-permute-start = (bf16[192,2,512]{2,1,0:T(2,128)(2,1)S(1)}, bf16[192,2,512]{2,1,0:T(2,128)(2,1)}, u32[]{:S(2)}, u32[]{:S(2)}) collective-permute-start(bf16[192,2,512]{2,1,0:T(2,128)(2,1)S(1)} %get-tuple-element.25), channel_id=1, source_target_pairs={{0,2},{2,4},{4,6},{6,0},{8,10},{10,12},{12,14},{14,8},{1,3},{3,5},... | collective-permute-start | bytes 1179656 | tf_op jit(solution)/shard_map/ppermute | solution.py:158
  28.7 4.4 %collective-permute-start.1 = (bf16[192,2,512]{2,1,0:T(2,128)(2,1)S(1)}, bf16[192,2,512]{2,1,0:T(2,128)(2,1)}, u32[]{:S(2)}, u32[]{:S(2)}) collective-permute-start(bf16[192,2,512]{2,1,0:T(2,128)(2,1)S(1)} %get-tuple-element.26), channel_id=1, source_target_pairs={{0,4},{2,6},{4,0},{6,2},{8,12},{10,14},{12,8},{14,10},{1,5},{3,7},... | collective-permute-start | bytes 1179656 | tf_op jit(solution)/shard_map/ppermute | solution.py:158
  33.0 3.1 %collective-permute-start.2 = (bf16[192,2,512]{2,1,0:T(2,128)(2,1)S(1)}, bf16[192,2,512]{2,1,0:T(2,128)(2,1)}, u32[]{:S(2)}, u32[]{:S(2)}) collective-permute-start(bf16[192,2,512]{2,1,0:T(2,128)(2,1)S(1)} %get-tuple-element.27), channel_id=1, source_target_pairs={{0,6},{2,0},{4,2},{6,4},{8,14},{10,8},{12,10},{14,12},{1,7},{3,1},... | collective-permute-start | bytes 1179656 | tf_op jit(solution)/shard_map/ppermute | solution.py:158
  36.1 12.8 %all-to-all-done = bf16[64,24,192]{2,1,0:T(8,128)(2,1)} async-done(((bf16[64,24,192]{2,1,0:T(8,128)(2,1)}), bf16[64,24,192]{2,1,0:T(8,128)(2,1)}, u32[]{:S(2)}, u32[]{:S(2)}) %all-to-all-start) | async-done | bytes 589856 | tf_op jit(solution)/shard_map/all_to_all | solution.py:150
  48.9 1.2 broadcast_select_fusion.1
  50.1 0.2 pad_maximum_fusion.refs_0_
  50.3 1.9 %collective-permute-start.7 = (bf16[768,384]{1,0:T(8,128)(2,1)S(1)}, bf16[768,384]{1,0:T(8,128)(2,1)S(1)}, u32[]{:S(2)}, u32[]{:S(2)}) collective-permute-start(bf16[768,384]{1,0:T(8,128)(2,1)S(1)} %pad_maximum_fusion.refs_0_), channel_id=1, source_target_pairs={{0,8},{8,0},{1,9},{9,1},{2,10},{10,2},{3,11},{11,3},{4,12},{12,4},... | collective-permute-start | bytes 1769480 | tf_op jit(solution)/shard_map/ppermute | solution.py:162
  52.2 3.4 %collective-permute-start.3 = (bf16[192,2,512]{2,1,0:T(2,128)(2,1)S(1)}, bf16[192,2,512]{2,1,0:T(2,128)(2,1)S(1)}, u32[]{:S(2)}, u32[]{:S(2)}) collective-permute-start(bf16[192,2,512]{2,1,0:T(2,128)(2,1)S(1)} %get-tuple-element.28), channel_id=1, source_target_pairs={{0,8},{2,10},{4,12},{6,14},{8,0},{10,2},{12,4},{14,6},{1,9},{3,11}... | collective-permute-start | bytes 1179656 | tf_op jit(solution)/shard_map/ppermute | solution.py:158
  55.6 2.9 %collective-permute-start.4 = (bf16[192,2,512]{2,1,0:T(2,128)(2,1)S(1)}, bf16[192,2,512]{2,1,0:T(2,128)(2,1)S(1)}, u32[]{:S(2)}, u32[]{:S(2)}) collective-permute-start(bf16[192,2,512]{2,1,0:T(2,128)(2,1)S(1)} %get-tuple-element.29), channel_id=1, source_target_pairs={{0,10},{2,12},{4,14},{6,8},{8,2},{10,4},{12,6},{14,0},{1,11},{3,13... | collective-permute-start | bytes 1179656 | tf_op jit(solution)/shard_map/ppermute | solution.py:158
  58.5 5.5 %collective-permute-start.5 = (bf16[192,2,512]{2,1,0:T(2,128)(2,1)S(1)}, bf16[192,2,512]{2,1,0:T(2,128)(2,1)S(1)}, u32[]{:S(2)}, u32[]{:S(2)}) collective-permute-start(bf16[192,2,512]{2,1,0:T(2,128)(2,1)S(1)} %get-tuple-element.30), channel_id=1, source_target_pairs={{0,12},{2,14},{4,8},{6,10},{8,4},{10,6},{12,0},{14,2},{1,13},{3,15... | collective-permute-start | bytes 1179656 | tf_op jit(solution)/shard_map/ppermute | solution.py:158
  64.0 2.8 %collective-permute-start.6 = (bf16[192,2,512]{2,1,0:T(2,128)(2,1)S(1)}, bf16[192,2,512]{2,1,0:T(2,128)(2,1)S(1)}, u32[]{:S(2)}, u32[]{:S(2)}) collective-permute-start(bf16[192,2,512]{2,1,0:T(2,128)(2,1)S(1)} %get-tuple-element.31), channel_id=1, source_target_pairs={{0,14},{2,8},{4,10},{6,12},{8,6},{10,0},{12,2},{14,4},{1,15},{3,9}... | collective-permute-start | bytes 1179656 | tf_op jit(solution)/shard_map/ppermute | solution.py:158
  66.8 8.2 %collective-permute-done.3 = bf16[192,2,512]{2,1,0:T(2,128)(2,1)S(1)} collective-permute-done((bf16[192,2,512]{2,1,0:T(2,128)(2,1)S(1)}, bf16[192,2,512]{2,1,0:T(2,128)(2,1)S(1)}, u32[]{:S(2)}, u32[]{:S(2)}) %collective-permute-start.3) | collective-permute-done | bytes 393248 | tf_op jit(solution)/shard_map/ppermute | solution.py:158
  75.0 10.6 %collective-permute-done.4 = bf16[192,2,512]{2,1,0:T(2,128)(2,1)S(1)} collective-permute-done((bf16[192,2,512]{2,1,0:T(2,128)(2,1)S(1)}, bf16[192,2,512]{2,1,0:T(2,128)(2,1)S(1)}, u32[]{:S(2)}, u32[]{:S(2)}) %collective-permute-start.4) | collective-permute-done | bytes 393248 | tf_op jit(solution)/shard_map/ppermute | solution.py:158
  85.6 8.7 %collective-permute-done.5 = bf16[192,2,512]{2,1,0:T(2,128)(2,1)S(1)} collective-permute-done((bf16[192,2,512]{2,1,0:T(2,128)(2,1)S(1)}, bf16[192,2,512]{2,1,0:T(2,128)(2,1)S(1)}, u32[]{:S(2)}, u32[]{:S(2)}) %collective-permute-start.5) | collective-permute-done | bytes 393248 | tf_op jit(solution)/shard_map/ppermute | solution.py:158
  94.3 6.9 %collective-permute-done.6 = bf16[192,2,512]{2,1,0:T(2,128)(2,1)S(1)} collective-permute-done((bf16[192,2,512]{2,1,0:T(2,128)(2,1)S(1)}, bf16[192,2,512]{2,1,0:T(2,128)(2,1)S(1)}, u32[]{:S(2)}, u32[]{:S(2)}) %collective-permute-start.6) | collective-permute-done | bytes 393248 | tf_op jit(solution)/shard_map/ppermute | solution.py:158
  101.3 1.0 copy.25
  102.4 1.0 copy.26
  103.4 1.0 copy.27
  104.9 3.3 %collective-permute-start.8 = (bf16[1536,1024]{1,0:T(8,128)(2,1)S(1)}, bf16[1536,1024]{1,0:T(8,128)(2,1)S(1)}, u32[]{:S(2)}, u32[]{:S(2)}) collective-permute-start(bf16[1536,1024]{1,0:T(8,128)(2,1)S(1)} %constant_dynamic-update-slice_fusion), channel_id=1, source_target_pairs={{0,1},{1,0},{2,3},{3,2},{4,5},{5,4},{6,7},{7,6},{8,9},{9,8},{10,11... | collective-permute-start | bytes 9437192 | tf_op jit(solution)/shard_map/ppermute | solution.py:165
  108.2 3.7 %collective-permute-start.9 = (bf16[768,384]{1,0:T(8,128)(2,1)S(1)}, bf16[768,384]{1,0:T(8,128)(2,1)S(1)}, u32[]{:S(2)}, u32[]{:S(2)}) collective-permute-start(bf16[768,384]{1,0:T(8,128)(2,1)S(1)} %pad_maximum_fusion.refs_0_), channel_id=1, source_target_pairs={{0,2},{2,4},{4,6},{6,0},{1,3},{3,5},{5,7},{7,1},{8,10},{10,12},{12... | collective-permute-start | bytes 1769480 | tf_op jit(solution)/shard_map/ppermute | solution.py:117
  111.9 2.7 %collective-permute-start.11 = (bf16[768,384]{1,0:T(8,128)(2,1)S(1)}, bf16[768,384]{1,0:T(8,128)(2,1)S(1)}, u32[]{:S(2)}, u32[]{:S(2)}) collective-permute-start(bf16[768,384]{1,0:T(8,128)(2,1)S(1)} %pad_maximum_fusion.refs_0_), channel_id=1, source_target_pairs={{0,6},{2,0},{4,2},{6,4},{1,7},{3,1},{5,3},{7,5},{8,14},{10,8},{12,... | collective-permute-start | bytes 1769480 | tf_op jit(solution)/shard_map/ppermute | solution.py:118
  114.7 2.5 %collective-permute-start.13 = (bf16[768,384]{1,0:T(8,128)(2,1)S(1)}, bf16[768,384]{1,0:T(8,128)(2,1)S(1)}, u32[]{:S(2)}, u32[]{:S(2)}) collective-permute-start(bf16[768,384]{1,0:T(8,128)(2,1)S(1)} %collective-permute-done.7.refs_3_), channel_id=1, source_target_pairs={{0,2},{2,4},{4,6},{6,0},{1,3},{3,5},{5,7},{7,1},{8,10},{10,12},{12... | collective-permute-start | bytes 1769480 | tf_op jit(solution)/shard_map/ppermute | solution.py:117
  117.2 4.0 %collective-permute-start.15 = (bf16[768,384]{1,0:T(8,128)(2,1)S(1)}, bf16[768,384]{1,0:T(8,128)(2,1)S(1)}, u32[]{:S(2)}, u32[]{:S(2)}) collective-permute-start(bf16[768,384]{1,0:T(8,128)(2,1)S(1)} %collective-permute-done.7.refs_3_), channel_id=1, source_target_pairs={{0,6},{2,0},{4,2},{6,4},{1,7},{3,1},{5,3},{7,5},{8,14},{10,8},{12,... | collective-permute-start | bytes 1769480 | tf_op jit(solution)/shard_map/ppermute | solution.py:118
  121.2 4.9 %collective-permute-done.9.refs_1_ = bf16[768,384]{1,0:T(8,128)(2,1)S(1)} collective-permute-done((bf16[768,384]{1,0:T(8,128)(2,1)S(1)}, bf16[768,384]{1,0:T(8,128)(2,1)S(1)}, u32[]{:S(2)}, u32[]{:S(2)}) %collective-permute-start.9) | collective-permute-done | bytes 589856 | tf_op jit(solution)/shard_map/ppermute | solution.py:117
  126.2 2.5 %collective-permute-start.10 = (bf16[384,384]{1,0:T(8,128)(2,1)S(1)}, bf16[384,384]{1,0:T(8,128)(2,1)S(1)}, u32[]{:S(2)}, u32[]{:S(2)}) collective-permute-start(bf16[384,384]{1,0:T(8,128)(2,1)S(1)} %slice.37), channel_id=1, source_target_pairs={{0,2},{2,4},{4,6},{6,0},{1,3},{3,5},{5,7},{7,1},{8,10},{10,12},{12... | collective-permute-start | bytes 884744 | tf_op jit(solution)/shard_map/ppermute | solution.py:120
  128.8 4.0 %collective-permute-start.12 = (bf16[384,384]{1,0:T(8,128)(2,1)S(1)}, bf16[384,384]{1,0:T(8,128)(2,1)S(1)}, u32[]{:S(2)}, u32[]{:S(2)}) collective-permute-start(bf16[384,384]{1,0:T(8,128)(2,1)S(1)} %slice.38), channel_id=1, source_target_pairs={{0,6},{2,0},{4,2},{6,4},{1,7},{3,1},{5,3},{7,5},{8,14},{10,8},{12,... | collective-permute-start | bytes 884744 | tf_op jit(solution)/shard_map/ppermute | solution.py:121
  132.8 6.0 %collective-permute-done.13.refs_4_ = bf16[768,384]{1,0:T(8,128)(2,1)S(1)} collective-permute-done((bf16[768,384]{1,0:T(8,128)(2,1)S(1)}, bf16[768,384]{1,0:T(8,128)(2,1)S(1)}, u32[]{:S(2)}, u32[]{:S(2)}) %collective-permute-start.13) | collective-permute-done | bytes 589856 | tf_op jit(solution)/shard_map/ppermute | solution.py:117
  138.8 2.5 %collective-permute-start.14 = (bf16[384,384]{1,0:T(8,128)(2,1)S(1)}, bf16[384,384]{1,0:T(8,128)(2,1)S(1)}, u32[]{:S(2)}, u32[]{:S(2)}) collective-permute-start(bf16[384,384]{1,0:T(8,128)(2,1)S(1)} %slice.39), channel_id=1, source_target_pairs={{0,2},{2,4},{4,6},{6,0},{1,3},{3,5},{5,7},{7,1},{8,10},{10,12},{12... | collective-permute-start | bytes 884744 | tf_op jit(solution)/shard_map/ppermute | solution.py:120
  141.4 4.0 %collective-permute-start.16 = (bf16[384,384]{1,0:T(8,128)(2,1)S(1)}, bf16[384,384]{1,0:T(8,128)(2,1)S(1)}, u32[]{:S(2)}, u32[]{:S(2)}) collective-permute-start(bf16[384,384]{1,0:T(8,128)(2,1)S(1)} %slice.40), channel_id=1, source_target_pairs={{0,6},{2,0},{4,2},{6,4},{1,7},{3,1},{5,3},{7,5},{8,14},{10,8},{12,... | collective-permute-start | bytes 884744 | tf_op jit(solution)/shard_map/ppermute | solution.py:121
  145.5 5.0 %shard_map.38.sums = f32[768,1024]{1,0:T(8,128)S(1)} custom-call(bf16[8,192,1024]{2,1,0:T(8,128)(2,1)S(1)} %bitcast.39, bf16[8,192,1024]{2,1,0:T(8,128)(2,1)S(1)} %bitcast.41, bf16[768,384]{1,0:T(8,128)(2,1)S(1)} %pad_maximum_fusion.refs_0_, bf16[768,384]{1,0:T(8,128)(2,1)S(1)} %collective-permute-done.9.refs_1_, ...), custom_call_target="tpu_custom_call" | custom-call | flops 2415919104 | bytes 6291456 | tf_op jit(solution)/shard_map/pallas_call | solution.py:103
  150.6 0.5 collective-permute-done.14.low1
  151.1 2.6 %collective-permute-done.16.high1 = bf16[384,384]{1,0:T(8,128)(2,1)S(1)} collective-permute-done((bf16[384,384]{1,0:T(8,128)(2,1)S(1)}, bf16[384,384]{1,0:T(8,128)(2,1)S(1)}, u32[]{:S(2)}, u32[]{:S(2)}) %collective-permute-start.16) | collective-permute-done | bytes 294944 | tf_op jit(solution)/shard_map/ppermute | solution.py:121
  153.7 1.8 shard_map.39
  155.6 31.4 %all_to_all.10 = bf16[64,24,256]{2,1,0:T(8,128)(2,1)S(1)} all-to-all(bf16[64,24,256]{2,1,0:T(8,128)(2,1)S(1)} %shard_map.39), channel_id=1, replica_groups=mesh['z'=8,'yh'=4,'yl'=2,'x'=4,'c'=2] {'yh','z','c'}, dimensions={0} | all-to-all | bytes 1572864 | tf_op jit(solution)/shard_map/all_to_all | solution.py:177
  186.9 0.4 copy.23
  187.3 0.5 convolution_convert_fusion
  187.8 1.2 reshape.112
  (40 shorter events, 1.3 us)
Async XLA Ops:
  0.0 3.1 %copy-start = (bf16[128,192]{0,1:T(8,128)(2,1)S(1)}, bf16[128,192]{0,1:T(8,128)(2,1)}, u32[]{:S(2)}) copy-start(bf16[128,192]{0,1:T(8,128)(2,1)} %param.3) | copy-start | bytes 147460
  4.4 44.5 %all-to-all-start = ((bf16[64,24,192]{2,1,0:T(8,128)(2,1)}), bf16[64,24,192]{2,1,0:T(8,128)(2,1)}, u32[]{:S(2)}, u32[]{:S(2)}) async-start(bf16[64,24,192]{2,1,0:T(8,128)(2,1)} %bitcast.3), calls=%async_computation | async-start | bytes 1572864 | tf_op jit(solution)/shard_map/all_to_all | solution.py:150
  22.2 1.9 %copy-start.1 = (bf16[1,192,2,4096]{3,2,1,0:T(2,128)(2,1)S(1)}, bf16[1,192,2,4096]{3,2,1,0:T(2,128)(2,1)}, u32[]{:S(2)}) copy-start(bf16[1,192,2,4096]{3,2,1,0:T(2,128)(2,1)} %w_ref.1) | copy-start | bytes 9437188
  25.5 30.1 %collective-permute-start = (bf16[192,2,512]{2,1,0:T(2,128)(2,1)S(1)}, bf16[192,2,512]{2,1,0:T(2,128)(2,1)}, u32[]{:S(2)}, u32[]{:S(2)}) collective-permute-start(bf16[192,2,512]{2,1,0:T(2,128)(2,1)S(1)} %get-tuple-element.25), channel_id=1, source_target_pairs={{0,2},{2,4},{4,6},{6,0},{8,10},{10,12},{12,14},{14,8},{1,3},{3,5},... | collective-permute-start | bytes 1179656 | tf_op jit(solution)/shard_map/ppermute | solution.py:158
  28.7 29.8 %collective-permute-start.1 = (bf16[192,2,512]{2,1,0:T(2,128)(2,1)S(1)}, bf16[192,2,512]{2,1,0:T(2,128)(2,1)}, u32[]{:S(2)}, u32[]{:S(2)}) collective-permute-start(bf16[192,2,512]{2,1,0:T(2,128)(2,1)S(1)} %get-tuple-element.26), channel_id=1, source_target_pairs={{0,4},{2,6},{4,0},{6,2},{8,12},{10,14},{12,8},{14,10},{1,5},{3,7},... | collective-permute-start | bytes 1179656 | tf_op jit(solution)/shard_map/ppermute | solution.py:158
  33.0 31.0 %collective-permute-start.2 = (bf16[192,2,512]{2,1,0:T(2,128)(2,1)S(1)}, bf16[192,2,512]{2,1,0:T(2,128)(2,1)}, u32[]{:S(2)}, u32[]{:S(2)}) collective-permute-start(bf16[192,2,512]{2,1,0:T(2,128)(2,1)S(1)} %get-tuple-element.27), channel_id=1, source_target_pairs={{0,6},{2,0},{4,2},{6,4},{8,14},{10,8},{12,10},{14,12},{1,7},{3,1},... | collective-permute-start | bytes 1179656 | tf_op jit(solution)/shard_map/ppermute | solution.py:158
  50.3 50.9 %collective-permute-start.7 = (bf16[768,384]{1,0:T(8,128)(2,1)S(1)}, bf16[768,384]{1,0:T(8,128)(2,1)S(1)}, u32[]{:S(2)}, u32[]{:S(2)}) collective-permute-start(bf16[768,384]{1,0:T(8,128)(2,1)S(1)} %pad_maximum_fusion.refs_0_), channel_id=1, source_target_pairs={{0,8},{8,0},{1,9},{9,1},{2,10},{10,2},{3,11},{11,3},{4,12},{12,4},... | collective-permute-start | bytes 1769480 | tf_op jit(solution)/shard_map/ppermute | solution.py:162
  52.2 22.8 %collective-permute-start.3 = (bf16[192,2,512]{2,1,0:T(2,128)(2,1)S(1)}, bf16[192,2,512]{2,1,0:T(2,128)(2,1)S(1)}, u32[]{:S(2)}, u32[]{:S(2)}) collective-permute-start(bf16[192,2,512]{2,1,0:T(2,128)(2,1)S(1)} %get-tuple-element.28), channel_id=1, source_target_pairs={{0,8},{2,10},{4,12},{6,14},{8,0},{10,2},{12,4},{14,6},{1,9},{3,11}... | collective-permute-start | bytes 1179656 | tf_op jit(solution)/shard_map/ppermute | solution.py:158
  55.6 30.0 %collective-permute-start.4 = (bf16[192,2,512]{2,1,0:T(2,128)(2,1)S(1)}, bf16[192,2,512]{2,1,0:T(2,128)(2,1)S(1)}, u32[]{:S(2)}, u32[]{:S(2)}) collective-permute-start(bf16[192,2,512]{2,1,0:T(2,128)(2,1)S(1)} %get-tuple-element.29), channel_id=1, source_target_pairs={{0,10},{2,12},{4,14},{6,8},{8,2},{10,4},{12,6},{14,0},{1,11},{3,13... | collective-permute-start | bytes 1179656 | tf_op jit(solution)/shard_map/ppermute | solution.py:158
  58.5 35.8 %collective-permute-start.5 = (bf16[192,2,512]{2,1,0:T(2,128)(2,1)S(1)}, bf16[192,2,512]{2,1,0:T(2,128)(2,1)S(1)}, u32[]{:S(2)}, u32[]{:S(2)}) collective-permute-start(bf16[192,2,512]{2,1,0:T(2,128)(2,1)S(1)} %get-tuple-element.30), channel_id=1, source_target_pairs={{0,12},{2,14},{4,8},{6,10},{8,4},{10,6},{12,0},{14,2},{1,13},{3,15... | collective-permute-start | bytes 1179656 | tf_op jit(solution)/shard_map/ppermute | solution.py:158
  64.0 37.2 %collective-permute-start.6 = (bf16[192,2,512]{2,1,0:T(2,128)(2,1)S(1)}, bf16[192,2,512]{2,1,0:T(2,128)(2,1)S(1)}, u32[]{:S(2)}, u32[]{:S(2)}) collective-permute-start(bf16[192,2,512]{2,1,0:T(2,128)(2,1)S(1)} %get-tuple-element.31), channel_id=1, source_target_pairs={{0,14},{2,8},{4,10},{6,12},{8,6},{10,0},{12,2},{14,4},{1,15},{3,9}... | collective-permute-start | bytes 1179656 | tf_op jit(solution)/shard_map/ppermute | solution.py:158
  104.9 40.6 %collective-permute-start.8 = (bf16[1536,1024]{1,0:T(8,128)(2,1)S(1)}, bf16[1536,1024]{1,0:T(8,128)(2,1)S(1)}, u32[]{:S(2)}, u32[]{:S(2)}) collective-permute-start(bf16[1536,1024]{1,0:T(8,128)(2,1)S(1)} %constant_dynamic-update-slice_fusion), channel_id=1, source_target_pairs={{0,1},{1,0},{2,3},{3,2},{4,5},{5,4},{6,7},{7,6},{8,9},{9,8},{10,11... | collective-permute-start | bytes 9437192 | tf_op jit(solution)/shard_map/ppermute | solution.py:165
  108.2 18.0 %collective-permute-start.9 = (bf16[768,384]{1,0:T(8,128)(2,1)S(1)}, bf16[768,384]{1,0:T(8,128)(2,1)S(1)}, u32[]{:S(2)}, u32[]{:S(2)}) collective-permute-start(bf16[768,384]{1,0:T(8,128)(2,1)S(1)} %pad_maximum_fusion.refs_0_), channel_id=1, source_target_pairs={{0,2},{2,4},{4,6},{6,0},{1,3},{3,5},{5,7},{7,1},{8,10},{10,12},{12... | collective-permute-start | bytes 1769480 | tf_op jit(solution)/shard_map/ppermute | solution.py:117
  111.9 16.8 %collective-permute-start.11 = (bf16[768,384]{1,0:T(8,128)(2,1)S(1)}, bf16[768,384]{1,0:T(8,128)(2,1)S(1)}, u32[]{:S(2)}, u32[]{:S(2)}) collective-permute-start(bf16[768,384]{1,0:T(8,128)(2,1)S(1)} %pad_maximum_fusion.refs_0_), channel_id=1, source_target_pairs={{0,6},{2,0},{4,2},{6,4},{1,7},{3,1},{5,3},{7,5},{8,14},{10,8},{12,... | collective-permute-start | bytes 1769480 | tf_op jit(solution)/shard_map/ppermute | solution.py:118
  114.7 24.1 %collective-permute-start.13 = (bf16[768,384]{1,0:T(8,128)(2,1)S(1)}, bf16[768,384]{1,0:T(8,128)(2,1)S(1)}, u32[]{:S(2)}, u32[]{:S(2)}) collective-permute-start(bf16[768,384]{1,0:T(8,128)(2,1)S(1)} %collective-permute-done.7.refs_3_), channel_id=1, source_target_pairs={{0,2},{2,4},{4,6},{6,0},{1,3},{3,5},{5,7},{7,1},{8,10},{10,12},{12... | collective-permute-start | bytes 1769480 | tf_op jit(solution)/shard_map/ppermute | solution.py:117
  117.2 24.1 %collective-permute-start.15 = (bf16[768,384]{1,0:T(8,128)(2,1)S(1)}, bf16[768,384]{1,0:T(8,128)(2,1)S(1)}, u32[]{:S(2)}, u32[]{:S(2)}) collective-permute-start(bf16[768,384]{1,0:T(8,128)(2,1)S(1)} %collective-permute-done.7.refs_3_), channel_id=1, source_target_pairs={{0,6},{2,0},{4,2},{6,4},{1,7},{3,1},{5,3},{7,5},{8,14},{10,8},{12,... | collective-permute-start | bytes 1769480 | tf_op jit(solution)/shard_map/ppermute | solution.py:118
  126.2 24.4 %collective-permute-start.10 = (bf16[384,384]{1,0:T(8,128)(2,1)S(1)}, bf16[384,384]{1,0:T(8,128)(2,1)S(1)}, u32[]{:S(2)}, u32[]{:S(2)}) collective-permute-start(bf16[384,384]{1,0:T(8,128)(2,1)S(1)} %slice.37), channel_id=1, source_target_pairs={{0,2},{2,4},{4,6},{6,0},{1,3},{3,5},{5,7},{7,1},{8,10},{10,12},{12... | collective-permute-start | bytes 884744 | tf_op jit(solution)/shard_map/ppermute | solution.py:120
  128.8 21.8 %collective-permute-start.12 = (bf16[384,384]{1,0:T(8,128)(2,1)S(1)}, bf16[384,384]{1,0:T(8,128)(2,1)S(1)}, u32[]{:S(2)}, u32[]{:S(2)}) collective-permute-start(bf16[384,384]{1,0:T(8,128)(2,1)S(1)} %slice.38), channel_id=1, source_target_pairs={{0,6},{2,0},{4,2},{6,4},{1,7},{3,1},{5,3},{7,5},{8,14},{10,8},{12,... | collective-permute-start | bytes 884744 | tf_op jit(solution)/shard_map/ppermute | solution.py:121
  138.8 12.2 %collective-permute-start.14 = (bf16[384,384]{1,0:T(8,128)(2,1)S(1)}, bf16[384,384]{1,0:T(8,128)(2,1)S(1)}, u32[]{:S(2)}, u32[]{:S(2)}) collective-permute-start(bf16[384,384]{1,0:T(8,128)(2,1)S(1)} %slice.39), channel_id=1, source_target_pairs={{0,2},{2,4},{4,6},{6,0},{1,3},{3,5},{5,7},{7,1},{8,10},{10,12},{12... | collective-permute-start | bytes 884744 | tf_op jit(solution)/shard_map/ppermute | solution.py:120
  141.4 12.3 %collective-permute-start.16 = (bf16[384,384]{1,0:T(8,128)(2,1)S(1)}, bf16[384,384]{1,0:T(8,128)(2,1)S(1)}, u32[]{:S(2)}, u32[]{:S(2)}) collective-permute-start(bf16[384,384]{1,0:T(8,128)(2,1)S(1)} %slice.40), channel_id=1, source_target_pairs={{0,6},{2,0},{4,2},{6,4},{1,7},{3,1},{5,3},{7,5},{8,14},{10,8},{12,... | collective-permute-start | bytes 884744 | tf_op jit(solution)/shard_map/ppermute | solution.py:121

commit v3 on v2

--- a/solution.py
+++ b/solution.py
@@ -95,7 +95,7 @@
             active = (gate / (1.0 + jnp.exp(-gate)) * up).astype(jnp.bfloat16)
             for j in range(BLOCK // n):
                 z, row = divmod(start // n + j, copies)
-                out[(row * zs + z) * cores + c] = active[j * n : (j + 1) * n]
+                out[(c * zs + z) * copies + row] = active[j * n : (j + 1) * n]
 
 
 def on_core(kernel, out_shape, *inputs):
@@ -137,7 +137,7 @@
     chosen = (flat_ids[:, None] == jnp.arange(E, dtype=jnp.int32)[None, :]).astype(jnp.int32)
     earlier = jnp.cumsum(chosen, axis=0) - chosen
     position = jnp.sum(earlier * chosen, axis=1)
-    slot_index = flat_ids * CAP + position
+    slot_index = flat_ids * part + position + (position >= part) * (E * part - part)
     slots = jnp.arange(E * CAP, dtype=jnp.int32)
     pick_table = (slot_index[:, None] == slots[None, :]).astype(jnp.bfloat16)
     token_table = pick_table.reshape(tok_count, TOP, E * CAP).sum(axis=1)
@@ -145,10 +145,10 @@
         token_table, tokens, (((0,), (0,)), ((), ())), preferred_element_type=jnp.float32
     ).astype(jnp.bfloat16)
 
-    sent = placed.reshape(zs, 1, cores, part, rows)
-    sent = jnp.broadcast_to(sent, (zs, copies, cores, part, rows)).reshape(-1, part, rows)
-    got = lax.all_to_all(sent, ("z", "yh", "c"), 0, 0, tiled=True)
-    got = got.reshape(zs * copies, cores, part, rows)
+    sent = placed.reshape(cores, zs, 1, part, rows)
+    sent = jnp.broadcast_to(sent, (cores, zs, copies, part, rows)).reshape(-1, part, rows)
+    got = lax.all_to_all(sent, ("c", "z", "yh"), 0, 0, tiled=True)
+    got = got.reshape(cores, zs * copies, part, rows)
 
     turn = jnp.arange(chips, dtype=jnp.int32)
     chip = lax.rem(side + turn // xs, yls) * xs + lax.rem(here + turn % xs, xs)
@@ -156,8 +156,8 @@
     moved = [pieces[0]]
     for s in range(1, chips):
         moved.append(lax.ppermute(pieces[s], CHIPS, chip_shift(s // xs, s % xs)))
-    mine = jnp.where(core == 0, got[:, 0], got[:, 1])
-    theirs = jnp.where(core == 0, got[:, 1], got[:, 0])
+    mine = jnp.where(core == 0, got[0], got[1])
+    theirs = jnp.where(core == 0, got[1], got[0])
     own = jnp.concatenate([mine, theirs], axis=-1).reshape(zs * copies * part, cores * rows)
     opposite = lax.ppermute(own, "yl", SWAP)
     moved, opposite = lax.optimization_barrier((moved, opposite))
@@ -174,8 +174,8 @@
     outgoing = on_core(hidden_kernel, active, w_mine, w_other, *near[3:], *far[3:], half_sums)
 
     pick_table, outgoing = lax.optimization_barrier((pick_table, outgoing))
-    returned = lax.all_to_all(outgoing, ("yh", "z", "c"), 0, 0, tiled=True)
-    grouped = returned.reshape(copies, E * CAP, half_width).transpose(1, 0, 2)
+    returned = lax.all_to_all(outgoing, ("c", "z", "yh"), 0, 0, tiled=True)
+    grouped = returned.reshape(cores * E, copies, part, half_width).transpose(0, 2, 1, 3)
     grouped = grouped.reshape(E * CAP, copies * half_width)
     hidden = jnp.dot(pick_table, grouped, preferred_element_type=jnp.float32).astype(jnp.bfloat16)
     return hidden.reshape(tok_count, TOP, copies, half_width)

time: 190 us -> 191 us (level)
  blocking collectives: 31.4 us -> 33.8 us
    all_to_all x1, blocking collectives: 31.4 us -> 33.8 us  [local(): returned = lax.all_to_all(outgoing, ('c', 'z', 'yh'), 0, 0, tiled=True)]
    unnamed x20 -> x21, local copies, waits for them, and re-layouts: 6.21 us -> 6.37 us
where the time goes in v3:
time: 191 us; the launch traced here: 190 us
  starting transfers between devices  74 us (39%)
  waiting for transfers between devices  59.9 us (31%)
  blocking collectives  33.8 us (18%)
  local copies, waits for them, and re-layouts  9.83 us (5%)
  Pallas kernels  8.32 us (4%)
  other arithmetic  3.04 us (2%)
    ppermute x7, waiting for transfers between devices, local(): moved.append(lax.ppermute(pieces[s], CHIPS, chip_shift(s // xs, s % xs)))  34.5 us
    all_to_all x1, blocking collectives, local(): returned = lax.all_to_all(outgoing, ('c', 'z', 'yh'), 0, 0, tiled=True)  33.8 us
    ppermute x7, starting transfers between devices, local(): moved.append(lax.ppermute(pieces[s], CHIPS, chip_shift(s // xs, s % xs)))  25.1 us
    all_to_all x1, starting transfers between devices, local(): got = lax.all_to_all(sent, ('c', 'z', 'yh'), 0, 0, tiled=True)  17.9 us
    all_to_all x1, waiting for transfers between devices, local(): got = lax.all_to_all(sent, ('c', 'z', 'yh'), 0, 0, tiled=True)  11.2 us
    ppermute x2, waiting for transfers between devices, gather_x(): low = lax.ppermute(block, 'x', shift('x', 1))  11 us
    ppermute x2, starting transfers between devices, gather_x(): far_b = lax.ppermute(high_part, 'x', shift('x', -1))  7.9 us
    pallas_call x2, Pallas kernels, on_core(): pl.pallas_call(kernel, out_shape=out_shape, in_specs=[vmem] * len(inputs)...  6.87 us
  transfers between devices with their start and end apart: 18, of which 9 were waited for; matrix products, arithmetic and copies ran while one was open for 1% of the time, Pallas kernels for 3%

profile of v3, /device:TPU:1, one launch (start us, length us, event | category | flops | bytes accessed | tf_op | source)
XLA Modules:
  0.0 190.0 jit_solution(10246507346963007259)
XLA Ops:
  0.0 0.8 copy.19
  1.1 0.6 reduce-window.6
  1.7 0.2 slice_reduce_fusion
  2.0 0.1 reduce_sum.24
  2.2 0.7 fusion.7
  3.1 0.2 convolution_convert_fusion.1
  3.4 1.0 broadcast_in_dim.5
  4.4 17.9 %all-to-all-start = ((bf16[64,24,192]{2,1,0:T(8,128)(2,1)}), bf16[64,24,192]{2,1,0:T(8,128)(2,1)}, u32[]{:S(2)}, u32[]{:S(2)}) async-start(bf16[64,24,192]{2,1,0:T(8,128)(2,1)} %bitcast.3), calls=%async_computation | async-start | bytes 1572864 | tf_op jit(solution)/shard_map/all_to_all | solution.py:150
  22.3 1.9 copy-done.1
  24.2 1.5 shard_map.37
  25.6 3.1 %collective-permute-start = (bf16[192,2,512]{2,1,0:T(2,128)(2,1)S(1)}, bf16[192,2,512]{2,1,0:T(2,128)(2,1)}, u32[]{:S(2)}, u32[]{:S(2)}) collective-permute-start(bf16[192,2,512]{2,1,0:T(2,128)(2,1)S(1)} %get-tuple-element.25), channel_id=1, source_target_pairs={{0,2},{2,4},{4,6},{6,0},{8,10},{10,12},{12,14},{14,8},{1,3},{3,5},... | collective-permute-start | bytes 1179656 | tf_op jit(solution)/shard_map/ppermute | solution.py:158
  28.8 4.4 %collective-permute-start.1 = (bf16[192,2,512]{2,1,0:T(2,128)(2,1)S(1)}, bf16[192,2,512]{2,1,0:T(2,128)(2,1)}, u32[]{:S(2)}, u32[]{:S(2)}) collective-permute-start(bf16[192,2,512]{2,1,0:T(2,128)(2,1)S(1)} %get-tuple-element.26), channel_id=1, source_target_pairs={{0,4},{2,6},{4,0},{6,2},{8,12},{10,14},{12,8},{14,10},{1,5},{3,7},... | collective-permute-start | bytes 1179656 | tf_op jit(solution)/shard_map/ppermute | solution.py:158
  33.1 3.1 %collective-permute-start.2 = (bf16[192,2,512]{2,1,0:T(2,128)(2,1)S(1)}, bf16[192,2,512]{2,1,0:T(2,128)(2,1)}, u32[]{:S(2)}, u32[]{:S(2)}) collective-permute-start(bf16[192,2,512]{2,1,0:T(2,128)(2,1)S(1)} %get-tuple-element.27), channel_id=1, source_target_pairs={{0,6},{2,0},{4,2},{6,4},{8,14},{10,8},{12,10},{14,12},{1,7},{3,1},... | collective-permute-start | bytes 1179656 | tf_op jit(solution)/shard_map/ppermute | solution.py:158
  36.2 11.2 %all-to-all-done = bf16[64,24,192]{2,1,0:T(8,128)(2,1)} async-done(((bf16[64,24,192]{2,1,0:T(8,128)(2,1)}), bf16[64,24,192]{2,1,0:T(8,128)(2,1)}, u32[]{:S(2)}, u32[]{:S(2)}) %all-to-all-start) | async-done | bytes 589856 | tf_op jit(solution)/shard_map/all_to_all | solution.py:150
  47.4 1.2 broadcast_select_fusion.1
  48.6 0.2 pad_maximum_fusion
  48.8 1.9 %collective-permute-start.7 = (bf16[768,384]{1,0:T(8,128)(2,1)S(1)}, bf16[768,384]{1,0:T(8,128)(2,1)S(1)}, u32[]{:S(2)}, u32[]{:S(2)}) collective-permute-start(bf16[768,384]{1,0:T(8,128)(2,1)S(1)} %bitcast.42), channel_id=1, source_target_pairs={{0,8},{8,0},{1,9},{9,1},{2,10},{10,2},{3,11},{11,3},{4,12},{12,4},... | collective-permute-start | bytes 1769480 | tf_op jit(solution)/shard_map/ppermute | solution.py:162
  50.7 3.4 %collective-permute-start.3 = (bf16[192,2,512]{2,1,0:T(2,128)(2,1)S(1)}, bf16[192,2,512]{2,1,0:T(2,128)(2,1)S(1)}, u32[]{:S(2)}, u32[]{:S(2)}) collective-permute-start(bf16[192,2,512]{2,1,0:T(2,128)(2,1)S(1)} %get-tuple-element.28), channel_id=1, source_target_pairs={{0,8},{2,10},{4,12},{6,14},{8,0},{10,2},{12,4},{14,6},{1,9},{3,11}... | collective-permute-start | bytes 1179656 | tf_op jit(solution)/shard_map/ppermute | solution.py:158
  54.1 2.8 %collective-permute-start.4 = (bf16[192,2,512]{2,1,0:T(2,128)(2,1)S(1)}, bf16[192,2,512]{2,1,0:T(2,128)(2,1)S(1)}, u32[]{:S(2)}, u32[]{:S(2)}) collective-permute-start(bf16[192,2,512]{2,1,0:T(2,128)(2,1)S(1)} %get-tuple-element.29), channel_id=1, source_target_pairs={{0,10},{2,12},{4,14},{6,8},{8,2},{10,4},{12,6},{14,0},{1,11},{3,13... | collective-permute-start | bytes 1179656 | tf_op jit(solution)/shard_map/ppermute | solution.py:158
  57.0 5.5 %collective-permute-start.5 = (bf16[192,2,512]{2,1,0:T(2,128)(2,1)S(1)}, bf16[192,2,512]{2,1,0:T(2,128)(2,1)S(1)}, u32[]{:S(2)}, u32[]{:S(2)}) collective-permute-start(bf16[192,2,512]{2,1,0:T(2,128)(2,1)S(1)} %get-tuple-element.30), channel_id=1, source_target_pairs={{0,12},{2,14},{4,8},{6,10},{8,4},{10,6},{12,0},{14,2},{1,13},{3,15... | collective-permute-start | bytes 1179656 | tf_op jit(solution)/shard_map/ppermute | solution.py:158
  62.5 2.8 %collective-permute-start.6 = (bf16[192,2,512]{2,1,0:T(2,128)(2,1)S(1)}, bf16[192,2,512]{2,1,0:T(2,128)(2,1)S(1)}, u32[]{:S(2)}, u32[]{:S(2)}) collective-permute-start(bf16[192,2,512]{2,1,0:T(2,128)(2,1)S(1)} %get-tuple-element.31), channel_id=1, source_target_pairs={{0,14},{2,8},{4,10},{6,12},{8,6},{10,0},{12,2},{14,4},{1,15},{3,9}... | collective-permute-start | bytes 1179656 | tf_op jit(solution)/shard_map/ppermute | solution.py:158
  65.3 8.3 %collective-permute-done.3 = bf16[192,2,512]{2,1,0:T(2,128)(2,1)S(1)} collective-permute-done((bf16[192,2,512]{2,1,0:T(2,128)(2,1)S(1)}, bf16[192,2,512]{2,1,0:T(2,128)(2,1)S(1)}, u32[]{:S(2)}, u32[]{:S(2)}) %collective-permute-start.3) | collective-permute-done | bytes 393248 | tf_op jit(solution)/shard_map/ppermute | solution.py:158
  73.6 10.6 %collective-permute-done.4 = bf16[192,2,512]{2,1,0:T(2,128)(2,1)S(1)} collective-permute-done((bf16[192,2,512]{2,1,0:T(2,128)(2,1)S(1)}, bf16[192,2,512]{2,1,0:T(2,128)(2,1)S(1)}, u32[]{:S(2)}, u32[]{:S(2)}) %collective-permute-start.4) | collective-permute-done | bytes 393248 | tf_op jit(solution)/shard_map/ppermute | solution.py:158
  84.2 8.7 %collective-permute-done.5 = bf16[192,2,512]{2,1,0:T(2,128)(2,1)S(1)} collective-permute-done((bf16[192,2,512]{2,1,0:T(2,128)(2,1)S(1)}, bf16[192,2,512]{2,1,0:T(2,128)(2,1)S(1)}, u32[]{:S(2)}, u32[]{:S(2)}) %collective-permute-start.5) | collective-permute-done | bytes 393248 | tf_op jit(solution)/shard_map/ppermute | solution.py:158
  92.9 6.9 %collective-permute-done.6 = bf16[192,2,512]{2,1,0:T(2,128)(2,1)S(1)} collective-permute-done((bf16[192,2,512]{2,1,0:T(2,128)(2,1)S(1)}, bf16[192,2,512]{2,1,0:T(2,128)(2,1)S(1)}, u32[]{:S(2)}, u32[]{:S(2)}) %collective-permute-start.6) | collective-permute-done | bytes 393248 | tf_op jit(solution)/shard_map/ppermute | solution.py:158
  99.9 1.0 copy.26
  100.9 1.0 copy.27
  102.0 1.0 copy.28
  103.5 3.2 %collective-permute-start.8 = (bf16[1536,1024]{1,0:T(8,128)(2,1)S(1)}, bf16[1536,1024]{1,0:T(8,128)(2,1)S(1)}, u32[]{:S(2)}, u32[]{:S(2)}) collective-permute-start(bf16[1536,1024]{1,0:T(8,128)(2,1)S(1)} %constant_dynamic-update-slice_fusion), channel_id=1, source_target_pairs={{0,1},{1,0},{2,3},{3,2},{4,5},{5,4},{6,7},{7,6},{8,9},{9,8},{10,11... | collective-permute-start | bytes 9437192 | tf_op jit(solution)/shard_map/ppermute | solution.py:165
  106.7 3.8 %collective-permute-start.9 = (bf16[768,384]{1,0:T(8,128)(2,1)S(1)}, bf16[768,384]{1,0:T(8,128)(2,1)S(1)}, u32[]{:S(2)}, u32[]{:S(2)}) collective-permute-start(bf16[768,384]{1,0:T(8,128)(2,1)S(1)} %bitcast.43), channel_id=1, source_target_pairs={{0,2},{2,4},{4,6},{6,0},{1,3},{3,5},{5,7},{7,1},{8,10},{10,12},{12... | collective-permute-start | bytes 1769480 | tf_op jit(solution)/shard_map/ppermute | solution.py:117
  110.4 2.7 %collective-permute-start.11 = (bf16[768,384]{1,0:T(8,128)(2,1)S(1)}, bf16[768,384]{1,0:T(8,128)(2,1)S(1)}, u32[]{:S(2)}, u32[]{:S(2)}) collective-permute-start(bf16[768,384]{1,0:T(8,128)(2,1)S(1)} %bitcast.44), channel_id=1, source_target_pairs={{0,6},{2,0},{4,2},{6,4},{1,7},{3,1},{5,3},{7,5},{8,14},{10,8},{12,... | collective-permute-start | bytes 1769480 | tf_op jit(solution)/shard_map/ppermute | solution.py:118
  113.2 2.5 %collective-permute-start.13 = (bf16[768,384]{1,0:T(8,128)(2,1)S(1)}, bf16[768,384]{1,0:T(8,128)(2,1)S(1)}, u32[]{:S(2)}, u32[]{:S(2)}) collective-permute-start(bf16[768,384]{1,0:T(8,128)(2,1)S(1)} %collective-permute-done.7.refs_3_), channel_id=1, source_target_pairs={{0,2},{2,4},{4,6},{6,0},{1,3},{3,5},{5,7},{7,1},{8,10},{10,12},{12... | collective-permute-start | bytes 1769480 | tf_op jit(solution)/shard_map/ppermute | solution.py:117
  115.7 3.9 %collective-permute-start.15 = (bf16[768,384]{1,0:T(8,128)(2,1)S(1)}, bf16[768,384]{1,0:T(8,128)(2,1)S(1)}, u32[]{:S(2)}, u32[]{:S(2)}) collective-permute-start(bf16[768,384]{1,0:T(8,128)(2,1)S(1)} %collective-permute-done.7.refs_3_), channel_id=1, source_target_pairs={{0,6},{2,0},{4,2},{6,4},{1,7},{3,1},{5,3},{7,5},{8,14},{10,8},{12,... | collective-permute-start | bytes 1769480 | tf_op jit(solution)/shard_map/ppermute | solution.py:118
  119.7 4.9 %collective-permute-done.9.refs_1_ = bf16[768,384]{1,0:T(8,128)(2,1)S(1)} collective-permute-done((bf16[768,384]{1,0:T(8,128)(2,1)S(1)}, bf16[768,384]{1,0:T(8,128)(2,1)S(1)}, u32[]{:S(2)}, u32[]{:S(2)}) %collective-permute-start.9) | collective-permute-done | bytes 589856 | tf_op jit(solution)/shard_map/ppermute | solution.py:117
  124.7 2.5 %collective-permute-start.10 = (bf16[384,384]{1,0:T(8,128)(2,1)S(1)}, bf16[384,384]{1,0:T(8,128)(2,1)S(1)}, u32[]{:S(2)}, u32[]{:S(2)}) collective-permute-start(bf16[384,384]{1,0:T(8,128)(2,1)S(1)} %slice.39), channel_id=1, source_target_pairs={{0,2},{2,4},{4,6},{6,0},{1,3},{3,5},{5,7},{7,1},{8,10},{10,12},{12... | collective-permute-start | bytes 884744 | tf_op jit(solution)/shard_map/ppermute | solution.py:120
  127.3 3.9 %collective-permute-start.12 = (bf16[384,384]{1,0:T(8,128)(2,1)S(1)}, bf16[384,384]{1,0:T(8,128)(2,1)S(1)}, u32[]{:S(2)}, u32[]{:S(2)}) collective-permute-start(bf16[384,384]{1,0:T(8,128)(2,1)S(1)} %slice.40), channel_id=1, source_target_pairs={{0,6},{2,0},{4,2},{6,4},{1,7},{3,1},{5,3},{7,5},{8,14},{10,8},{12,... | collective-permute-start | bytes 884744 | tf_op jit(solution)/shard_map/ppermute | solution.py:121
  131.2 6.0 %collective-permute-done.13.refs_4_ = bf16[768,384]{1,0:T(8,128)(2,1)S(1)} collective-permute-done((bf16[768,384]{1,0:T(8,128)(2,1)S(1)}, bf16[768,384]{1,0:T(8,128)(2,1)S(1)}, u32[]{:S(2)}, u32[]{:S(2)}) %collective-permute-start.13) | collective-permute-done | bytes 589856 | tf_op jit(solution)/shard_map/ppermute | solution.py:117
  137.3 2.5 %collective-permute-start.14 = (bf16[384,384]{1,0:T(8,128)(2,1)S(1)}, bf16[384,384]{1,0:T(8,128)(2,1)S(1)}, u32[]{:S(2)}, u32[]{:S(2)}) collective-permute-start(bf16[384,384]{1,0:T(8,128)(2,1)S(1)} %slice.41), channel_id=1, source_target_pairs={{0,2},{2,4},{4,6},{6,0},{1,3},{3,5},{5,7},{7,1},{8,10},{10,12},{12... | collective-permute-start | bytes 884744 | tf_op jit(solution)/shard_map/ppermute | solution.py:120
  139.9 3.9 %collective-permute-start.16 = (bf16[384,384]{1,0:T(8,128)(2,1)S(1)}, bf16[384,384]{1,0:T(8,128)(2,1)S(1)}, u32[]{:S(2)}, u32[]{:S(2)}) collective-permute-start(bf16[384,384]{1,0:T(8,128)(2,1)S(1)} %slice.42), channel_id=1, source_target_pairs={{0,6},{2,0},{4,2},{6,4},{1,7},{3,1},{5,3},{7,5},{8,14},{10,8},{12,... | collective-permute-start | bytes 884744 | tf_op jit(solution)/shard_map/ppermute | solution.py:121
  144.0 5.0 %shard_map.38.sums = f32[768,1024]{1,0:T(8,128)S(1)} custom-call(bf16[8,192,1024]{2,1,0:T(8,128)(2,1)S(1)} %bitcast.38, bf16[8,192,1024]{2,1,0:T(8,128)(2,1)S(1)} %bitcast.40, bf16[768,384]{1,0:T(8,128)(2,1)S(1)} %bitcast.45, bf16[768,384]{1,0:T(8,128)(2,1)S(1)} %collective-permute-done.9.refs_1_, bf16[768,384]{1,0:T(8,128)(2,1)S(1)} %collective-permute-done.11.refs_2_, ...), custom_call_target="tpu_custom_call" | custom-call | flops 2415919104 | bytes 6291456 | tf_op jit(solution)/shard_map/pallas_call | solution.py:103
  149.1 0.5 collective-permute-done.14.low1
  149.5 2.6 %collective-permute-done.16.high1 = bf16[384,384]{1,0:T(8,128)(2,1)S(1)} collective-permute-done((bf16[384,384]{1,0:T(8,128)(2,1)S(1)}, bf16[384,384]{1,0:T(8,128)(2,1)S(1)}, u32[]{:S(2)}, u32[]{:S(2)}) %collective-permute-start.16) | collective-permute-done | bytes 294944 | tf_op jit(solution)/shard_map/ppermute | solution.py:121
  152.2 1.8 shard_map.39
  154.0 33.8 %all_to_all.10 = bf16[64,24,256]{2,1,0:T(8,128)(2,1)S(1)} all-to-all(bf16[64,24,256]{2,1,0:T(8,128)(2,1)S(1)} %shard_map.39), channel_id=1, replica_groups=mesh['z'=8,'yh'=4,'yl'=2,'x'=4,'c'=2] {'c','z','yh'}, dimensions={0} | all-to-all | bytes 1572864 | tf_op jit(solution)/shard_map/all_to_all | solution.py:177
  187.8 0.4 copy.24
  188.2 0.2 copy.33
  188.4 0.4 convolution_convert_fusion
  188.8 1.2 reshape.109
  (41 shorter events, 1.4 us)
Async XLA Ops:
  0.0 3.1 %copy-start = (bf16[128,192]{0,1:T(8,128)(2,1)S(1)}, bf16[128,192]{0,1:T(8,128)(2,1)}, u32[]{:S(2)}) copy-start(bf16[128,192]{0,1:T(8,128)(2,1)} %param.3) | copy-start | bytes 147460
  4.4 43.0 %all-to-all-start = ((bf16[64,24,192]{2,1,0:T(8,128)(2,1)}), bf16[64,24,192]{2,1,0:T(8,128)(2,1)}, u32[]{:S(2)}, u32[]{:S(2)}) async-start(bf16[64,24,192]{2,1,0:T(8,128)(2,1)} %bitcast.3), calls=%async_computation | async-start | bytes 1572864 | tf_op jit(solution)/shard_map/all_to_all | solution.py:150
  22.3 1.9 copy-start.1
  25.6 28.5 %collective-permute-start = (bf16[192,2,512]{2,1,0:T(2,128)(2,1)S(1)}, bf16[192,2,512]{2,1,0:T(2,128)(2,1)}, u32[]{:S(2)}, u32[]{:S(2)}) collective-permute-start(bf16[192,2,512]{2,1,0:T(2,128)(2,1)S(1)} %get-tuple-element.25), channel_id=1, source_target_pairs={{0,2},{2,4},{4,6},{6,0},{8,10},{10,12},{12,14},{14,8},{1,3},{3,5},... | collective-permute-start | bytes 1179656 | tf_op jit(solution)/shard_map/ppermute | solution.py:158
  28.8 28.2 %collective-permute-start.1 = (bf16[192,2,512]{2,1,0:T(2,128)(2,1)S(1)}, bf16[192,2,512]{2,1,0:T(2,128)(2,1)}, u32[]{:S(2)}, u32[]{:S(2)}) collective-permute-start(bf16[192,2,512]{2,1,0:T(2,128)(2,1)S(1)} %get-tuple-element.26), channel_id=1, source_target_pairs={{0,4},{2,6},{4,0},{6,2},{8,12},{10,14},{12,8},{14,10},{1,5},{3,7},... | collective-permute-start | bytes 1179656 | tf_op jit(solution)/shard_map/ppermute | solution.py:158
  33.1 29.4 %collective-permute-start.2 = (bf16[192,2,512]{2,1,0:T(2,128)(2,1)S(1)}, bf16[192,2,512]{2,1,0:T(2,128)(2,1)}, u32[]{:S(2)}, u32[]{:S(2)}) collective-permute-start(bf16[192,2,512]{2,1,0:T(2,128)(2,1)S(1)} %get-tuple-element.27), channel_id=1, source_target_pairs={{0,6},{2,0},{4,2},{6,4},{8,14},{10,8},{12,10},{14,12},{1,7},{3,1},... | collective-permute-start | bytes 1179656 | tf_op jit(solution)/shard_map/ppermute | solution.py:158
  48.8 51.0 %collective-permute-start.7 = (bf16[768,384]{1,0:T(8,128)(2,1)S(1)}, bf16[768,384]{1,0:T(8,128)(2,1)S(1)}, u32[]{:S(2)}, u32[]{:S(2)}) collective-permute-start(bf16[768,384]{1,0:T(8,128)(2,1)S(1)} %bitcast.42), channel_id=1, source_target_pairs={{0,8},{8,0},{1,9},{9,1},{2,10},{10,2},{3,11},{11,3},{4,12},{12,4},... | collective-permute-start | bytes 1769480 | tf_op jit(solution)/shard_map/ppermute | solution.py:162
  50.7 22.9 %collective-permute-start.3 = (bf16[192,2,512]{2,1,0:T(2,128)(2,1)S(1)}, bf16[192,2,512]{2,1,0:T(2,128)(2,1)S(1)}, u32[]{:S(2)}, u32[]{:S(2)}) collective-permute-start(bf16[192,2,512]{2,1,0:T(2,128)(2,1)S(1)} %get-tuple-element.28), channel_id=1, source_target_pairs={{0,8},{2,10},{4,12},{6,14},{8,0},{10,2},{12,4},{14,6},{1,9},{3,11}... | collective-permute-start | bytes 1179656 | tf_op jit(solution)/shard_map/ppermute | solution.py:158
  54.1 30.1 %collective-permute-start.4 = (bf16[192,2,512]{2,1,0:T(2,128)(2,1)S(1)}, bf16[192,2,512]{2,1,0:T(2,128)(2,1)S(1)}, u32[]{:S(2)}, u32[]{:S(2)}) collective-permute-start(bf16[192,2,512]{2,1,0:T(2,128)(2,1)S(1)} %get-tuple-element.29), channel_id=1, source_target_pairs={{0,10},{2,12},{4,14},{6,8},{8,2},{10,4},{12,6},{14,0},{1,11},{3,13... | collective-permute-start | bytes 1179656 | tf_op jit(solution)/shard_map/ppermute | solution.py:158
  57.0 35.9 %collective-permute-start.5 = (bf16[192,2,512]{2,1,0:T(2,128)(2,1)S(1)}, bf16[192,2,512]{2,1,0:T(2,128)(2,1)S(1)}, u32[]{:S(2)}, u32[]{:S(2)}) collective-permute-start(bf16[192,2,512]{2,1,0:T(2,128)(2,1)S(1)} %get-tuple-element.30), channel_id=1, source_target_pairs={{0,12},{2,14},{4,8},{6,10},{8,4},{10,6},{12,0},{14,2},{1,13},{3,15... | collective-permute-start | bytes 1179656 | tf_op jit(solution)/shard_map/ppermute | solution.py:158
  62.5 37.3 %collective-permute-start.6 = (bf16[192,2,512]{2,1,0:T(2,128)(2,1)S(1)}, bf16[192,2,512]{2,1,0:T(2,128)(2,1)S(1)}, u32[]{:S(2)}, u32[]{:S(2)}) collective-permute-start(bf16[192,2,512]{2,1,0:T(2,128)(2,1)S(1)} %get-tuple-element.31), channel_id=1, source_target_pairs={{0,14},{2,8},{4,10},{6,12},{8,6},{10,0},{12,2},{14,4},{1,15},{3,9}... | collective-permute-start | bytes 1179656 | tf_op jit(solution)/shard_map/ppermute | solution.py:158
  103.5 40.5 %collective-permute-start.8 = (bf16[1536,1024]{1,0:T(8,128)(2,1)S(1)}, bf16[1536,1024]{1,0:T(8,128)(2,1)S(1)}, u32[]{:S(2)}, u32[]{:S(2)}) collective-permute-start(bf16[1536,1024]{1,0:T(8,128)(2,1)S(1)} %constant_dynamic-update-slice_fusion), channel_id=1, source_target_pairs={{0,1},{1,0},{2,3},{3,2},{4,5},{5,4},{6,7},{7,6},{8,9},{9,8},{10,11... | collective-permute-start | bytes 9437192 | tf_op jit(solution)/shard_map/ppermute | solution.py:165
  106.7 18.0 %collective-permute-start.9 = (bf16[768,384]{1,0:T(8,128)(2,1)S(1)}, bf16[768,384]{1,0:T(8,128)(2,1)S(1)}, u32[]{:S(2)}, u32[]{:S(2)}) collective-permute-start(bf16[768,384]{1,0:T(8,128)(2,1)S(1)} %bitcast.43), channel_id=1, source_target_pairs={{0,2},{2,4},{4,6},{6,0},{1,3},{3,5},{5,7},{7,1},{8,10},{10,12},{12... | collective-permute-start | bytes 1769480 | tf_op jit(solution)/shard_map/ppermute | solution.py:117
  110.4 16.8 %collective-permute-start.11 = (bf16[768,384]{1,0:T(8,128)(2,1)S(1)}, bf16[768,384]{1,0:T(8,128)(2,1)S(1)}, u32[]{:S(2)}, u32[]{:S(2)}) collective-permute-start(bf16[768,384]{1,0:T(8,128)(2,1)S(1)} %bitcast.44), channel_id=1, source_target_pairs={{0,6},{2,0},{4,2},{6,4},{1,7},{3,1},{5,3},{7,5},{8,14},{10,8},{12,... | collective-permute-start | bytes 1769480 | tf_op jit(solution)/shard_map/ppermute | solution.py:118
  113.2 24.1 %collective-permute-start.13 = (bf16[768,384]{1,0:T(8,128)(2,1)S(1)}, bf16[768,384]{1,0:T(8,128)(2,1)S(1)}, u32[]{:S(2)}, u32[]{:S(2)}) collective-permute-start(bf16[768,384]{1,0:T(8,128)(2,1)S(1)} %collective-permute-done.7.refs_3_), channel_id=1, source_target_pairs={{0,2},{2,4},{4,6},{6,0},{1,3},{3,5},{5,7},{7,1},{8,10},{10,12},{12... | collective-permute-start | bytes 1769480 | tf_op jit(solution)/shard_map/ppermute | solution.py:117
  115.7 24.1 %collective-permute-start.15 = (bf16[768,384]{1,0:T(8,128)(2,1)S(1)}, bf16[768,384]{1,0:T(8,128)(2,1)S(1)}, u32[]{:S(2)}, u32[]{:S(2)}) collective-permute-start(bf16[768,384]{1,0:T(8,128)(2,1)S(1)} %collective-permute-done.7.refs_3_), channel_id=1, source_target_pairs={{0,6},{2,0},{4,2},{6,4},{1,7},{3,1},{5,3},{7,5},{8,14},{10,8},{12,... | collective-permute-start | bytes 1769480 | tf_op jit(solution)/shard_map/ppermute | solution.py:118
  124.7 24.4 %collective-permute-start.10 = (bf16[384,384]{1,0:T(8,128)(2,1)S(1)}, bf16[384,384]{1,0:T(8,128)(2,1)S(1)}, u32[]{:S(2)}, u32[]{:S(2)}) collective-permute-start(bf16[384,384]{1,0:T(8,128)(2,1)S(1)} %slice.39), channel_id=1, source_target_pairs={{0,2},{2,4},{4,6},{6,0},{1,3},{3,5},{5,7},{7,1},{8,10},{10,12},{12... | collective-permute-start | bytes 884744 | tf_op jit(solution)/shard_map/ppermute | solution.py:120
  127.3 21.8 %collective-permute-start.12 = (bf16[384,384]{1,0:T(8,128)(2,1)S(1)}, bf16[384,384]{1,0:T(8,128)(2,1)S(1)}, u32[]{:S(2)}, u32[]{:S(2)}) collective-permute-start(bf16[384,384]{1,0:T(8,128)(2,1)S(1)} %slice.40), channel_id=1, source_target_pairs={{0,6},{2,0},{4,2},{6,4},{1,7},{3,1},{5,3},{7,5},{8,14},{10,8},{12,... | collective-permute-start | bytes 884744 | tf_op jit(solution)/shard_map/ppermute | solution.py:121
  137.3 12.2 %collective-permute-start.14 = (bf16[384,384]{1,0:T(8,128)(2,1)S(1)}, bf16[384,384]{1,0:T(8,128)(2,1)S(1)}, u32[]{:S(2)}, u32[]{:S(2)}) collective-permute-start(bf16[384,384]{1,0:T(8,128)(2,1)S(1)} %slice.41), channel_id=1, source_target_pairs={{0,2},{2,4},{4,6},{6,0},{1,3},{3,5},{5,7},{7,1},{8,10},{10,12},{12... | collective-permute-start | bytes 884744 | tf_op jit(solution)/shard_map/ppermute | solution.py:120
  139.9 12.3 %collective-permute-start.16 = (bf16[384,384]{1,0:T(8,128)(2,1)S(1)}, bf16[384,384]{1,0:T(8,128)(2,1)S(1)}, u32[]{:S(2)}, u32[]{:S(2)}) collective-permute-start(bf16[384,384]{1,0:T(8,128)(2,1)S(1)} %slice.42), channel_id=1, source_target_pairs={{0,6},{2,0},{4,2},{6,4},{1,7},{3,1},{5,3},{7,5},{8,14},{10,8},{12,... | collective-permute-start | bytes 884744 | tf_op jit(solution)/shard_map/ppermute | solution.py:121

commit v4 on v3

--- a/solution.py
+++ b/solution.py
@@ -112,14 +112,15 @@
     )(*inputs)
 
 
-def gather_x(block):
+def gather_x(block, later):
     half = block.shape[0] // 2
     low = lax.ppermute(block, "x", shift("x", 1))
     high = lax.ppermute(block, "x", shift("x", -1))
     low_part, high_part = low[:half], high[half:]
+    low_part, high_part, later = lax.optimization_barrier((low_part, high_part, later))
     far_a = lax.ppermute(low_part, "x", shift("x", 1))
     far_b = lax.ppermute(high_part, "x", shift("x", -1))
-    return block, low, high, far_a, far_b
+    return (block, low, high, far_a, far_b), later
 
 
 def local(tokens, expert_ids, joined_weight):
@@ -160,14 +161,13 @@
     theirs = jnp.where(core == 0, got[1], got[0])
     own = jnp.concatenate([mine, theirs], axis=-1).reshape(zs * copies * part, cores * rows)
     opposite = lax.ppermute(own, "yl", SWAP)
-    moved, opposite = lax.optimization_barrier((moved, opposite))
+    near, moved = gather_x(own, moved)
     w_mine = jnp.concatenate([m.reshape(rows, 2 * chip_width) for m in moved], axis=0)
     w_other = lax.ppermute(w_mine, "c", SWAP)
     shape = (chips, rows, 2 * chip_width)
     w_mine, w_other = w_mine.reshape(shape), w_other.reshape(shape)
 
-    near = gather_x(own)
-    far = gather_x(opposite)
+    far, _ = gather_x(opposite, ())
     sums = jax.ShapeDtypeStruct((own.shape[0], 2 * chip_width), jnp.float32)
     half_sums = on_core(near_kernel, sums, w_mine, w_other, *near[:3], *far[:3])
     active = jax.ShapeDtypeStruct((zs * copies * cores, part, half_width), jnp.bfloat16)

time: 191 us -> 209 us (1.094)
  waiting for transfers between devices: 59.9 us -> 81.6 us
  local copies, waits for them, and re-layouts: 9.83 us -> 4.97 us
  blocking collectives: 33.8 us -> 37.3 us
  starting transfers between devices: 74 us -> 71.6 us
    ppermute x1, waiting for transfers between devices: 0.01 us -> 14.8 us  [local(): opposite = lax.ppermute(own, 'yl', SWAP)]
    all_to_all x1, waiting for transfers between devices: 11.2 us -> 25.1 us  [local(): got = lax.all_to_all(sent, ('c', 'z', 'yh'), 0, 0, tiled=True)]
    ppermute x2, waiting for transfers between devices: 11 us -> 3.34 us  [gather_x(): low = lax.ppermute(block, 'x', shift('x', 1))]
    unnamed x21, local copies, waits for them, and re-layouts: 6.37 us -> 1.5 us
    ppermute x7, starting transfers between devices: 25.1 us -> 20.6 us  [local(): moved.append(lax.ppermute(pieces[s], CHIPS, chip_shift(s // xs, s % xs)))]
    ppermute x2, waiting for transfers between devices: 0.01 us -> 3.81 us  [gather_x(): high = lax.ppermute(block, 'x', shift('x', -1))]
    all_to_all x1, blocking collectives: 33.8 us -> 37.3 us  [local(): returned = lax.all_to_all(outgoing, ('c', 'z', 'yh'), 0, 0, tiled=True)]
    ppermute x2, waiting for transfers between devices: 2.65 us -> 0.01 us  [gather_x(): far_b = lax.ppermute(high_part, 'x', shift('x', -1))]
  transfers between devices with their start and end apart: 18 -> 18, of which waited for: 9 -> 9; matrix products, arithmetic and copies ran while one was open for 1% -> 0% of each run, Pallas kernels for 3% -> 3%
where the time goes in v4:
time: 209 us; the launch traced here: 208 us
  waiting for transfers between devices  81.6 us (39%)
  starting transfers between devices  71.6 us (34%)
  blocking collectives  37.3 us (18%)
  Pallas kernels  8.34 us (4%)
  local copies, waits for them, and re-layouts  4.97 us (2%)
  other arithmetic  3.19 us (2%)
    all_to_all x1, blocking collectives, local(): returned = lax.all_to_all(outgoing, ('c', 'z', 'yh'), 0, 0, tiled=True)  37.3 us
    ppermute x7, waiting for transfers between devices, local(): moved.append(lax.ppermute(pieces[s], CHIPS, chip_shift(s // xs, s % xs)))  34.4 us
    all_to_all x1, waiting for transfers between devices, local(): got = lax.all_to_all(sent, ('c', 'z', 'yh'), 0, 0, tiled=True)  25.1 us
    ppermute x7, starting transfers between devices, local(): moved.append(lax.ppermute(pieces[s], CHIPS, chip_shift(s // xs, s % xs)))  20.6 us
    all_to_all x1, starting transfers between devices, local(): got = lax.all_to_all(sent, ('c', 'z', 'yh'), 0, 0, tiled=True)  17.9 us
    ppermute x1, waiting for transfers between devices, local(): opposite = lax.ppermute(own, 'yl', SWAP)  14.8 us
    ppermute x2, starting transfers between devices, gather_x(): low = lax.ppermute(block, 'x', shift('x', 1))  8.9 us
    pallas_call x2, Pallas kernels, on_core(): pl.pallas_call(kernel, out_shape=out_shape, in_specs=[vmem] * len(inputs)...  6.87 us
  transfers between devices with their start and end apart: 18, of which 9 were waited for; matrix products, arithmetic and copies ran while one was open for 0% of the time, Pallas kernels for 3%

profile of v4, /device:TPU:1, one launch (start us, length us, event | category | flops | bytes accessed | tf_op | source)
XLA Modules:
  0.0 208.1 jit_solution(3494068068497796669)
XLA Ops:
  0.0 0.8 copy.19
  0.8 0.1 eq.52
  0.9 0.1 reshape.93
  1.1 0.6 reduce-window.6
  1.7 0.2 slice_reduce_fusion
  2.0 0.1 reduce_sum.24
  2.2 0.9 fusion.7
  3.1 0.1 fusion.2
  3.2 0.2 convolution_convert_fusion.1
  3.4 0.1 copy.23
  3.6 1.0 broadcast_in_dim.5
  4.5 17.9 %all-to-all-start = ((bf16[64,24,192]{2,1,0:T(8,128)(2,1)}), bf16[64,24,192]{2,1,0:T(8,128)(2,1)}, u32[]{:S(2)}, u32[]{:S(2)}) async-start(bf16[64,24,192]{2,1,0:T(8,128)(2,1)} %bitcast.50), calls=%async_computation | async-start | bytes 1572864 | tf_op jit(solution)/shard_map/all_to_all | solution.py:151
  22.4 25.1 %all-to-all-done = bf16[64,24,192]{2,1,0:T(8,128)(2,1)} async-done(((bf16[64,24,192]{2,1,0:T(8,128)(2,1)}), bf16[64,24,192]{2,1,0:T(8,128)(2,1)}, u32[]{:S(2)}, u32[]{:S(2)}) %all-to-all-start) | async-done | bytes 589856 | tf_op jit(solution)/shard_map/all_to_all | solution.py:151
  47.6 1.2 broadcast_select_fusion.1
  48.7 0.2 pad_maximum_fusion
  48.9 3.1 %collective-permute-start = (bf16[768,384]{1,0:T(8,128)(2,1)S(1)}, bf16[768,384]{1,0:T(8,128)(2,1)S(1)}, u32[]{:S(2)}, u32[]{:S(2)}) collective-permute-start(bf16[768,384]{1,0:T(8,128)(2,1)S(1)} %bitcast.42), channel_id=1, source_target_pairs={{0,2},{2,4},{4,6},{6,0},{1,3},{3,5},{5,7},{7,1},{8,10},{10,12},{12... | collective-permute-start | bytes 1769480 | tf_op jit(solution)/shard_map/ppermute | solution.py:117
  52.1 3.4 %collective-permute-start.1 = (bf16[768,384]{1,0:T(8,128)(2,1)S(1)}, bf16[768,384]{1,0:T(8,128)(2,1)S(1)}, u32[]{:S(2)}, u32[]{:S(2)}) collective-permute-start(bf16[768,384]{1,0:T(8,128)(2,1)S(1)} %bitcast.43), channel_id=1, source_target_pairs={{0,6},{2,0},{4,2},{6,4},{1,7},{3,1},{5,3},{7,5},{8,14},{10,8},{12,... | collective-permute-start | bytes 1769480 | tf_op jit(solution)/shard_map/ppermute | solution.py:118
  55.5 1.5 shard_map.37
  57.0 1.9 collective-permute-start.2
  58.9 4.3 %collective-permute-start.3 = (bf16[192,2,512]{2,1,0:T(2,128)(2,1)S(1)}, bf16[192,2,512]{2,1,0:T(2,128)(2,1)S(1)}, u32[]{:S(2)}, u32[]{:S(2)}) collective-permute-start(bf16[192,2,512]{2,1,0:T(2,128)(2,1)S(1)} %get-tuple-element.29), channel_id=1, source_target_pairs={{0,4},{2,6},{4,0},{6,2},{8,12},{10,14},{12,8},{14,10},{1,5},{3,7},... | collective-permute-start | bytes 1179656 | tf_op jit(solution)/shard_map/ppermute | solution.py:159
  63.2 3.1 %collective-permute-start.4 = (bf16[192,2,512]{2,1,0:T(2,128)(2,1)S(1)}, bf16[192,2,512]{2,1,0:T(2,128)(2,1)S(1)}, u32[]{:S(2)}, u32[]{:S(2)}) collective-permute-start(bf16[192,2,512]{2,1,0:T(2,128)(2,1)S(1)} %get-tuple-element.30), channel_id=1, source_target_pairs={{0,6},{2,0},{4,2},{6,4},{8,14},{10,8},{12,10},{14,12},{1,7},{3,1},... | collective-permute-start | bytes 1179656 | tf_op jit(solution)/shard_map/ppermute | solution.py:159
  66.3 8.6 %collective-permute-done.2 = bf16[192,2,512]{2,1,0:T(2,128)(2,1)S(1)} collective-permute-done((bf16[192,2,512]{2,1,0:T(2,128)(2,1)S(1)}, bf16[192,2,512]{2,1,0:T(2,128)(2,1)S(1)}, u32[]{:S(2)}, u32[]{:S(2)}) %collective-permute-start.2) | collective-permute-done | bytes 393248 | tf_op jit(solution)/shard_map/ppermute | solution.py:159
  75.0 1.9 collective-permute-start.5
  76.9 7.5 %collective-permute-done.3 = bf16[192,2,512]{2,1,0:T(2,128)(2,1)S(1)} collective-permute-done((bf16[192,2,512]{2,1,0:T(2,128)(2,1)S(1)}, bf16[192,2,512]{2,1,0:T(2,128)(2,1)S(1)}, u32[]{:S(2)}, u32[]{:S(2)}) %collective-permute-start.3) | collective-permute-done | bytes 393248 | tf_op jit(solution)/shard_map/ppermute | solution.py:159
  84.4 1.9 collective-permute-start.6
  86.3 1.9 collective-permute-start.7
  88.2 5.5 %collective-permute-start.8 = (bf16[192,2,512]{2,1,0:T(2,128)(2,1)S(1)}, bf16[192,2,512]{2,1,0:T(2,128)(2,1)S(1)}, u32[]{:S(2)}, u32[]{:S(2)}) collective-permute-start(bf16[192,2,512]{2,1,0:T(2,128)(2,1)S(1)} %get-tuple-element.34), channel_id=1, source_target_pairs={{0,14},{2,8},{4,10},{6,12},{8,6},{10,0},{12,2},{14,4},{1,15},{3,9}... | collective-permute-start | bytes 1179656 | tf_op jit(solution)/shard_map/ppermute | solution.py:159
  93.8 5.3 %collective-permute-done.6 = bf16[192,2,512]{2,1,0:T(2,128)(2,1)S(1)} collective-permute-done((bf16[192,2,512]{2,1,0:T(2,128)(2,1)S(1)}, bf16[192,2,512]{2,1,0:T(2,128)(2,1)S(1)}, u32[]{:S(2)}, u32[]{:S(2)}) %collective-permute-start.6) | collective-permute-done | bytes 393248 | tf_op jit(solution)/shard_map/ppermute | solution.py:159
  99.1 6.2 %collective-permute-done.7 = bf16[192,2,512]{2,1,0:T(2,128)(2,1)S(1)} collective-permute-done((bf16[192,2,512]{2,1,0:T(2,128)(2,1)S(1)}, bf16[192,2,512]{2,1,0:T(2,128)(2,1)S(1)}, u32[]{:S(2)}, u32[]{:S(2)}) %collective-permute-start.7) | collective-permute-done | bytes 393248 | tf_op jit(solution)/shard_map/ppermute | solution.py:159
  105.3 6.8 %collective-permute-done.8 = bf16[192,2,512]{2,1,0:T(2,128)(2,1)S(1)} collective-permute-done((bf16[192,2,512]{2,1,0:T(2,128)(2,1)S(1)}, bf16[192,2,512]{2,1,0:T(2,128)(2,1)S(1)}, u32[]{:S(2)}, u32[]{:S(2)}) %collective-permute-start.8) | collective-permute-done | bytes 393248 | tf_op jit(solution)/shard_map/ppermute | solution.py:159
  112.8 4.1 %collective-permute-start.9 = (bf16[1536,1024]{1,0:T(8,128)(2,1)S(1)}, bf16[1536,1024]{1,0:T(8,128)(2,1)S(1)}, u32[]{:S(2)}, u32[]{:S(2)}) collective-permute-start(bf16[1536,1024]{1,0:T(8,128)(2,1)S(1)} %constant_dynamic-update-slice_fusion), channel_id=1, source_target_pairs={{0,1},{1,0},{2,3},{3,2},{4,5},{5,4},{6,7},{7,6},{8,9},{9,8},{10,11... | collective-permute-start | bytes 9437192 | tf_op jit(solution)/shard_map/ppermute | solution.py:166
  116.9 1.9 collective-permute-start.12
  118.8 14.8 %collective-permute-done.12.refs_3_ = bf16[768,384]{1,0:T(8,128)(2,1)S(1)} collective-permute-done((bf16[768,384]{1,0:T(8,128)(2,1)S(1)}, bf16[768,384]{1,0:T(8,128)(2,1)S(1)}, u32[]{:S(2)}, u32[]{:S(2)}) %collective-permute-start.12) | collective-permute-done | bytes 589856 | tf_op jit(solution)/shard_map/ppermute | solution.py:163
  133.7 5.8 %collective-permute-start.13 = (bf16[768,384]{1,0:T(8,128)(2,1)S(1)}, bf16[768,384]{1,0:T(8,128)(2,1)S(1)}, u32[]{:S(2)}, u32[]{:S(2)}) collective-permute-start(bf16[768,384]{1,0:T(8,128)(2,1)S(1)} %collective-permute-done.12.refs_3_), channel_id=1, source_target_pairs={{0,2},{2,4},{4,6},{6,0},{1,3},{3,5},{5,7},{7,1},{8,10},{10,12},{12... | collective-permute-start | bytes 1769480 | tf_op jit(solution)/shard_map/ppermute | solution.py:117
  139.4 1.9 collective-permute-start.14
  141.4 3.4 %collective-permute-start.10 = (bf16[384,384]{1,0:T(8,128)(2,1)S(1)}, bf16[384,384]{1,0:T(8,128)(2,1)S(1)}, u32[]{:S(2)}, u32[]{:S(2)}) collective-permute-start(bf16[384,384]{1,0:T(8,128)(2,1)S(1)} %slice.39), channel_id=1, source_target_pairs={{0,2},{2,4},{4,6},{6,0},{1,3},{3,5},{5,7},{7,1},{8,10},{10,12},{12... | collective-permute-start | bytes 884744 | tf_op jit(solution)/shard_map/ppermute | solution.py:121
  144.7 3.1 %collective-permute-start.11 = (bf16[384,384]{1,0:T(8,128)(2,1)S(1)}, bf16[384,384]{1,0:T(8,128)(2,1)S(1)}, u32[]{:S(2)}, u32[]{:S(2)}) collective-permute-start(bf16[384,384]{1,0:T(8,128)(2,1)S(1)} %slice.40), channel_id=1, source_target_pairs={{0,6},{2,0},{4,2},{6,4},{1,7},{3,1},{5,3},{7,5},{8,14},{10,8},{12,... | collective-permute-start | bytes 884744 | tf_op jit(solution)/shard_map/ppermute | solution.py:122
  147.9 3.3 %collective-permute-done.13.refs_4_ = bf16[768,384]{1,0:T(8,128)(2,1)S(1)} collective-permute-done((bf16[768,384]{1,0:T(8,128)(2,1)S(1)}, bf16[768,384]{1,0:T(8,128)(2,1)S(1)}, u32[]{:S(2)}, u32[]{:S(2)}) %collective-permute-start.13) | collective-permute-done | bytes 589856 | tf_op jit(solution)/shard_map/ppermute | solution.py:117
  151.3 3.8 %collective-permute-done.14.refs_5_ = bf16[768,384]{1,0:T(8,128)(2,1)S(1)} collective-permute-done((bf16[768,384]{1,0:T(8,128)(2,1)S(1)}, bf16[768,384]{1,0:T(8,128)(2,1)S(1)}, u32[]{:S(2)}, u32[]{:S(2)}) %collective-permute-start.14) | collective-permute-done | bytes 589856 | tf_op jit(solution)/shard_map/ppermute | solution.py:118
  155.1 3.0 %collective-permute-start.15 = (bf16[384,384]{1,0:T(8,128)(2,1)S(1)}, bf16[384,384]{1,0:T(8,128)(2,1)S(1)}, u32[]{:S(2)}, u32[]{:S(2)}) collective-permute-start(bf16[384,384]{1,0:T(8,128)(2,1)S(1)} %slice.41), channel_id=1, source_target_pairs={{0,2},{2,4},{4,6},{6,0},{1,3},{3,5},{5,7},{7,1},{8,10},{10,12},{12... | collective-permute-start | bytes 884744 | tf_op jit(solution)/shard_map/ppermute | solution.py:121
  158.1 3.5 %collective-permute-start.16 = (bf16[384,384]{1,0:T(8,128)(2,1)S(1)}, bf16[384,384]{1,0:T(8,128)(2,1)S(1)}, u32[]{:S(2)}, u32[]{:S(2)}) collective-permute-start(bf16[384,384]{1,0:T(8,128)(2,1)S(1)} %slice.42), channel_id=1, source_target_pairs={{0,6},{2,0},{4,2},{6,4},{1,7},{3,1},{5,3},{7,5},{8,14},{10,8},{12,... | collective-permute-start | bytes 884744 | tf_op jit(solution)/shard_map/ppermute | solution.py:122
  161.7 5.0 %shard_map.38.sums = f32[768,1024]{1,0:T(8,128)S(1)} custom-call(bf16[8,192,1024]{2,1,0:T(8,128)(2,1)S(1)} %bitcast.38, bf16[8,192,1024]{2,1,0:T(8,128)(2,1)S(1)} %bitcast.40, bf16[768,384]{1,0:T(8,128)(2,1)S(1)} %bitcast.45, bf16[768,384]{1,0:T(8,128)(2,1)S(1)} %collective-permute-done.refs_1_, bf16[768,384]{1,0:T(8,128)(2,1)S(1)} %collective-permute-done.1.refs_2_, ...), custom_call_target="tpu_custom_call" | custom-call | flops 2415919104 | bytes 6291456 | tf_op jit(solution)/shard_map/pallas_call | solution.py:103
  166.8 1.8 shard_map.39
  168.7 37.3 %all_to_all.10 = bf16[64,24,256]{2,1,0:T(8,128)(2,1)S(1)} all-to-all(bf16[64,24,256]{2,1,0:T(8,128)(2,1)S(1)} %shard_map.39), channel_id=1, replica_groups=mesh['z'=8,'yh'=4,'yl'=2,'x'=4,'c'=2] {'c','z','yh'}, dimensions={0} | all-to-all | bytes 1572864 | tf_op jit(solution)/shard_map/all_to_all | solution.py:177
  205.9 0.4 copy.24
  206.3 0.2 copy.33
  206.5 0.4 convolution_convert_fusion
  206.9 1.2 reshape.109
  (41 shorter events, 1.0 us)
Async XLA Ops:
  0.0 3.2 %copy-start = (bf16[128,192]{0,1:T(8,128)(2,1)S(1)}, bf16[128,192]{0,1:T(8,128)(2,1)}, u32[]{:S(2)}) copy-start(bf16[128,192]{0,1:T(8,128)(2,1)} %param.3) | copy-start | bytes 147460
  2.2 53.2 %copy-start.1 = (bf16[1,192,2,4096]{3,2,1,0:T(2,128)(2,1)S(1)}, bf16[1,192,2,4096]{3,2,1,0:T(2,128)(2,1)}, u32[]{:S(2)}) copy-start(bf16[1,192,2,4096]{3,2,1,0:T(2,128)(2,1)} %w_ref.1) | copy-start | bytes 9437188
  4.5 43.0 %all-to-all-start = ((bf16[64,24,192]{2,1,0:T(8,128)(2,1)}), bf16[64,24,192]{2,1,0:T(8,128)(2,1)}, u32[]{:S(2)}, u32[]{:S(2)}) async-start(bf16[64,24,192]{2,1,0:T(8,128)(2,1)} %bitcast.50), calls=%async_computation | async-start | bytes 1572864 | tf_op jit(solution)/shard_map/all_to_all | solution.py:151
  48.9 37.4 %collective-permute-start = (bf16[768,384]{1,0:T(8,128)(2,1)S(1)}, bf16[768,384]{1,0:T(8,128)(2,1)S(1)}, u32[]{:S(2)}, u32[]{:S(2)}) collective-permute-start(bf16[768,384]{1,0:T(8,128)(2,1)S(1)} %bitcast.42), channel_id=1, source_target_pairs={{0,2},{2,4},{4,6},{6,0},{1,3},{3,5},{5,7},{7,1},{8,10},{10,12},{12... | collective-permute-start | bytes 1769480 | tf_op jit(solution)/shard_map/ppermute | solution.py:117
  52.1 36.2 %collective-permute-start.1 = (bf16[768,384]{1,0:T(8,128)(2,1)S(1)}, bf16[768,384]{1,0:T(8,128)(2,1)S(1)}, u32[]{:S(2)}, u32[]{:S(2)}) collective-permute-start(bf16[768,384]{1,0:T(8,128)(2,1)S(1)} %bitcast.43), channel_id=1, source_target_pairs={{0,6},{2,0},{4,2},{6,4},{1,7},{3,1},{5,3},{7,5},{8,14},{10,8},{12,... | collective-permute-start | bytes 1769480 | tf_op jit(solution)/shard_map/ppermute | solution.py:118
  57.0 18.0 %collective-permute-start.2 = (bf16[192,2,512]{2,1,0:T(2,128)(2,1)S(1)}, bf16[192,2,512]{2,1,0:T(2,128)(2,1)S(1)}, u32[]{:S(2)}, u32[]{:S(2)}) collective-permute-start(bf16[192,2,512]{2,1,0:T(2,128)(2,1)S(1)} %get-tuple-element.28), channel_id=1, source_target_pairs={{0,2},{2,4},{4,6},{6,0},{8,10},{10,12},{12,14},{14,8},{1,3},{3,5},... | collective-permute-start | bytes 1179656 | tf_op jit(solution)/shard_map/ppermute | solution.py:159
  58.9 25.5 %collective-permute-start.3 = (bf16[192,2,512]{2,1,0:T(2,128)(2,1)S(1)}, bf16[192,2,512]{2,1,0:T(2,128)(2,1)S(1)}, u32[]{:S(2)}, u32[]{:S(2)}) collective-permute-start(bf16[192,2,512]{2,1,0:T(2,128)(2,1)S(1)} %get-tuple-element.29), channel_id=1, source_target_pairs={{0,4},{2,6},{4,0},{6,2},{8,12},{10,14},{12,8},{14,10},{1,5},{3,7},... | collective-permute-start | bytes 1179656 | tf_op jit(solution)/shard_map/ppermute | solution.py:159
  63.2 30.6 %collective-permute-start.4 = (bf16[192,2,512]{2,1,0:T(2,128)(2,1)S(1)}, bf16[192,2,512]{2,1,0:T(2,128)(2,1)S(1)}, u32[]{:S(2)}, u32[]{:S(2)}) collective-permute-start(bf16[192,2,512]{2,1,0:T(2,128)(2,1)S(1)} %get-tuple-element.30), channel_id=1, source_target_pairs={{0,6},{2,0},{4,2},{6,4},{8,14},{10,8},{12,10},{14,12},{1,7},{3,1},... | collective-permute-start | bytes 1179656 | tf_op jit(solution)/shard_map/ppermute | solution.py:159
  75.0 18.9 %collective-permute-start.5 = (bf16[192,2,512]{2,1,0:T(2,128)(2,1)S(1)}, bf16[192,2,512]{2,1,0:T(2,128)(2,1)S(1)}, u32[]{:S(2)}, u32[]{:S(2)}) collective-permute-start(bf16[192,2,512]{2,1,0:T(2,128)(2,1)S(1)} %get-tuple-element.31), channel_id=1, source_target_pairs={{0,8},{2,10},{4,12},{6,14},{8,0},{10,2},{12,4},{14,6},{1,9},{3,11}... | collective-permute-start | bytes 1179656 | tf_op jit(solution)/shard_map/ppermute | solution.py:159
  84.4 14.8 %collective-permute-start.6 = (bf16[192,2,512]{2,1,0:T(2,128)(2,1)S(1)}, bf16[192,2,512]{2,1,0:T(2,128)(2,1)S(1)}, u32[]{:S(2)}, u32[]{:S(2)}) collective-permute-start(bf16[192,2,512]{2,1,0:T(2,128)(2,1)S(1)} %get-tuple-element.32), channel_id=1, source_target_pairs={{0,10},{2,12},{4,14},{6,8},{8,2},{10,4},{12,6},{14,0},{1,11},{3,13... | collective-permute-start | bytes 1179656 | tf_op jit(solution)/shard_map/ppermute | solution.py:159
  86.3 19.0 %collective-permute-start.7 = (bf16[192,2,512]{2,1,0:T(2,128)(2,1)S(1)}, bf16[192,2,512]{2,1,0:T(2,128)(2,1)S(1)}, u32[]{:S(2)}, u32[]{:S(2)}) collective-permute-start(bf16[192,2,512]{2,1,0:T(2,128)(2,1)S(1)} %get-tuple-element.33), channel_id=1, source_target_pairs={{0,12},{2,14},{4,8},{6,10},{8,4},{10,6},{12,0},{14,2},{1,13},{3,15... | collective-permute-start | bytes 1179656 | tf_op jit(solution)/shard_map/ppermute | solution.py:159
  88.2 23.9 %collective-permute-start.8 = (bf16[192,2,512]{2,1,0:T(2,128)(2,1)S(1)}, bf16[192,2,512]{2,1,0:T(2,128)(2,1)S(1)}, u32[]{:S(2)}, u32[]{:S(2)}) collective-permute-start(bf16[192,2,512]{2,1,0:T(2,128)(2,1)S(1)} %get-tuple-element.34), channel_id=1, source_target_pairs={{0,14},{2,8},{4,10},{6,12},{8,6},{10,0},{12,2},{14,4},{1,15},{3,9}... | collective-permute-start | bytes 1179656 | tf_op jit(solution)/shard_map/ppermute | solution.py:159
  112.8 48.9 %collective-permute-start.9 = (bf16[1536,1024]{1,0:T(8,128)(2,1)S(1)}, bf16[1536,1024]{1,0:T(8,128)(2,1)S(1)}, u32[]{:S(2)}, u32[]{:S(2)}) collective-permute-start(bf16[1536,1024]{1,0:T(8,128)(2,1)S(1)} %constant_dynamic-update-slice_fusion), channel_id=1, source_target_pairs={{0,1},{1,0},{2,3},{3,2},{4,5},{5,4},{6,7},{7,6},{8,9},{9,8},{10,11... | collective-permute-start | bytes 9437192 | tf_op jit(solution)/shard_map/ppermute | solution.py:166
  116.9 16.8 %collective-permute-start.12 = (bf16[768,384]{1,0:T(8,128)(2,1)S(1)}, bf16[768,384]{1,0:T(8,128)(2,1)S(1)}, u32[]{:S(2)}, u32[]{:S(2)}) collective-permute-start(bf16[768,384]{1,0:T(8,128)(2,1)S(1)} %bitcast.44), channel_id=1, source_target_pairs={{0,8},{8,0},{1,9},{9,1},{2,10},{10,2},{3,11},{11,3},{4,12},{12,4},... | collective-permute-start | bytes 1769480 | tf_op jit(solution)/shard_map/ppermute | solution.py:163
  133.7 17.6 %collective-permute-start.13 = (bf16[768,384]{1,0:T(8,128)(2,1)S(1)}, bf16[768,384]{1,0:T(8,128)(2,1)S(1)}, u32[]{:S(2)}, u32[]{:S(2)}) collective-permute-start(bf16[768,384]{1,0:T(8,128)(2,1)S(1)} %collective-permute-done.12.refs_3_), channel_id=1, source_target_pairs={{0,2},{2,4},{4,6},{6,0},{1,3},{3,5},{5,7},{7,1},{8,10},{10,12},{12... | collective-permute-start | bytes 1769480 | tf_op jit(solution)/shard_map/ppermute | solution.py:117
  139.4 15.6 %collective-permute-start.14 = (bf16[768,384]{1,0:T(8,128)(2,1)S(1)}, bf16[768,384]{1,0:T(8,128)(2,1)S(1)}, u32[]{:S(2)}, u32[]{:S(2)}) collective-permute-start(bf16[768,384]{1,0:T(8,128)(2,1)S(1)} %collective-permute-done.12.refs_3_), channel_id=1, source_target_pairs={{0,6},{2,0},{4,2},{6,4},{1,7},{3,1},{5,3},{7,5},{8,14},{10,8},{12,... | collective-permute-start | bytes 1769480 | tf_op jit(solution)/shard_map/ppermute | solution.py:118
  141.4 25.4 %collective-permute-start.10 = (bf16[384,384]{1,0:T(8,128)(2,1)S(1)}, bf16[384,384]{1,0:T(8,128)(2,1)S(1)}, u32[]{:S(2)}, u32[]{:S(2)}) collective-permute-start(bf16[384,384]{1,0:T(8,128)(2,1)S(1)} %slice.39), channel_id=1, source_target_pairs={{0,2},{2,4},{4,6},{6,0},{1,3},{3,5},{5,7},{7,1},{8,10},{10,12},{12... | collective-permute-start | bytes 884744 | tf_op jit(solution)/shard_map/ppermute | solution.py:121
  144.7 22.0 %collective-permute-start.11 = (bf16[384,384]{1,0:T(8,128)(2,1)S(1)}, bf16[384,384]{1,0:T(8,128)(2,1)S(1)}, u32[]{:S(2)}, u32[]{:S(2)}) collective-permute-start(bf16[384,384]{1,0:T(8,128)(2,1)S(1)} %slice.40), channel_id=1, source_target_pairs={{0,6},{2,0},{4,2},{6,4},{1,7},{3,1},{5,3},{7,5},{8,14},{10,8},{12,... | collective-permute-start | bytes 884744 | tf_op jit(solution)/shard_map/ppermute | solution.py:122
  155.1 11.7 %collective-permute-start.15 = (bf16[384,384]{1,0:T(8,128)(2,1)S(1)}, bf16[384,384]{1,0:T(8,128)(2,1)S(1)}, u32[]{:S(2)}, u32[]{:S(2)}) collective-permute-start(bf16[384,384]{1,0:T(8,128)(2,1)S(1)} %slice.41), channel_id=1, source_target_pairs={{0,2},{2,4},{4,6},{6,0},{1,3},{3,5},{5,7},{7,1},{8,10},{10,12},{12... | collective-permute-start | bytes 884744 | tf_op jit(solution)/shard_map/ppermute | solution.py:121
  158.1 8.7 %collective-permute-start.16 = (bf16[384,384]{1,0:T(8,128)(2,1)S(1)}, bf16[384,384]{1,0:T(8,128)(2,1)S(1)}, u32[]{:S(2)}, u32[]{:S(2)}) collective-permute-start(bf16[384,384]{1,0:T(8,128)(2,1)S(1)} %slice.42), channel_id=1, source_target_pairs={{0,6},{2,0},{4,2},{6,4},{1,7},{3,1},{5,3},{7,5},{8,14},{10,8},{12,... | collective-permute-start | bytes 884744 | tf_op jit(solution)/shard_map/ppermute | solution.py:122
